TPU v7x, 256 devices: a whole 4x4x8 slice. The times are simulated.
256 devices in a mesh: rows: 64 (over z, y, core), grp: 4 (over x).
Axes of the slice: x: 4, y: 4, z: 8, core: 2. Of those that a mesh axis runs over, the one named last changes fastest.
Arguments:
- cholesky_vectors: bfloat16 [524288, 2048], P(('rows', 'grp'))
- integral_columns: float32 [524288, 64], P(('rows', 'grp'))
- residual_diag: float32 [524288], P(('rows', 'grp')), may hold values from 40 to 120
- slot_pair_block: int32 [4096], P(('rows', 'grp')), may hold values from 0 to 4095, as said below
- block_live: int32 [4096], P(('rows', 'grp')), may hold values from 0 to 1, as said below
- pivots: int32 [64], replicated, may hold values from 0 to 524287, as said below
Outputs:
- new_columns: float32 [524288, 64], P(('rows', 'grp'))
- relative_diag: float32 [524288], P(('rows', 'grp'))
- peak: float32 [], replicated
Inputs may be any that keep to these rules, and one draw needn't show every extreme that they name: `slot_pair_block`: each block number appears once. `block_live`: slots s * 16 to s * 16 + 15 are those of device s; each device has 1 to 12 surviving slots, and some device has exactly 12. Distinct; every pivot lies in a surviving slot; each device's slots hold at most 1 pivots, and some device holds exactly 1.
All inputs are finite; a program needn't handle non-finite values.
Results may differ from a plain program's by a relative error of at most 0.0003.
Values sent between devices are 32-bit elements; how exact they have to be, the bound alone decides.
No kernel may reach another device: no remote copies, remote signals or barrier semaphores. Data moves between devices by JAX's collectives and lax.ppermute only.
A program may use at most 64 MiB of HBM per device.

v0:
```python
import jax
import jax.numpy as jnp
from jax import lax
from jax.sharding import Mesh
from jax.sharding import PartitionSpec as P

ROWS = ("rows_0", "rows_1", "rows_2")
ROWS_GRP = ("rows_0", "rows_1", "rows_2", "grp")


def copy_for_each(value, axis):
    copies = jnp.broadcast_to(value, (lax.axis_size(axis), *value.shape))
    return lax.all_to_all(copies, axis, split_axis=0, concat_axis=0, tiled=True)


def joined_along(blocks, dim):
    blocks = jnp.moveaxis(blocks, 0, dim)
    dims = blocks.shape
    return blocks.reshape(*dims[:dim], dims[dim] * dims[dim + 1], *dims[dim + 2 :])


def gathered_by_axis(value, axes, dim):
    far, near = axes
    blocks = copy_for_each(copy_for_each(value, far), near)
    return joined_along(blocks.swapaxes(0, 1).reshape(-1, *value.shape), dim)


def in_one_piece(arrays, axis, dim, along):
    ends, at = ([], 0)
    for a in arrays[:-1]:
        at += a.shape[along]
        ends.append(at)
    both = jnp.concatenate(arrays, axis=along)
    return tuple(jnp.split(gathered_by_axis(both, axis, dim), ends, axis=along))


def taken_together(value, axis):
    return copy_for_each(value, axis).max(axis=0)


def one_axis_at_a_time(value, axes):
    far, near = axes
    nearer = taken_together(value, near)
    return taken_together(nearer, far)


def on_device(
    cholesky_vectors, integral_columns, residual_diag, slot_pair_block, block_live, pivots
):
    slots = slot_pair_block.shape[0]
    total_rows = cholesky_vectors.shape[0]
    block_rows = total_rows // slots
    piv_count = pivots.shape[0]
    holders = lax.axis_size(ROWS) * lax.axis_size("grp")
    per_holder = max(1, piv_count // holders)
    pivot_group = pivots // block_rows
    pivot_offset = pivots % block_rows
    matches = pivot_group[:, None] == slot_pair_block[None, :]
    is_owned = jnp.any(matches, axis=1)
    local_slot = jnp.argmax(matches.astype(jnp.int32), axis=1)
    local_row = local_slot * block_rows + pivot_offset
    own_vectors = jnp.where(
        is_owned[:, None], cholesky_vectors[local_row], jnp.zeros((), jnp.bfloat16)
    )
    own_block = jnp.where(is_owned[:, None], integral_columns[local_row], 0.0)
    pivot_rank = jnp.cumsum(is_owned.astype(jnp.int32)) - 1
    selector = (pivot_rank[None, :] == jnp.arange(per_holder)[:, None]) & is_owned[None, :]
    packed_vectors = jnp.dot(
        selector.astype(jnp.bfloat16), own_vectors, preferred_element_type=jnp.float32
    )
    packed_block = jnp.dot(selector.astype(jnp.float32), own_block, precision=lax.Precision.HIGHEST)
    packed_ids = jnp.where(
        jnp.any(selector, axis=1),
        jnp.sum(jnp.where(selector, jnp.arange(piv_count)[None, :], 0), axis=1),
        -1,
    )
    all_vectors, all_blocks, all_ids = (
        *in_one_piece(
            (packed_vectors, packed_block), (("rows_0", "rows_1"), ("rows_2", "grp")), 0, 1
        ),
        gathered_by_axis(packed_ids, (("rows_0", "rows_1"), ("rows_2", "grp")), 0),
    )
    placing = (all_ids[None, :] == jnp.arange(piv_count)[:, None]).astype(jnp.float32)
    picked_wide = jnp.dot(placing, all_vectors, precision=lax.Precision.HIGHEST)
    pivot_block = jnp.dot(placing, all_blocks, precision=lax.Precision.HIGHEST)
    gram = jnp.dot(picked_wide, picked_wide.T, precision=lax.Precision.HIGHEST)
    lower_factor = jnp.linalg.cholesky(pivot_block - gram)
    picked = picked_wide.astype(jnp.bfloat16)
    row_live = jnp.repeat(block_live, block_rows) > 0
    remain = integral_columns - jnp.dot(
        cholesky_vectors, picked.T, preferred_element_type=jnp.float32
    )
    columns = lax.linalg.triangular_solve(
        lower_factor, remain, left_side=False, lower=True, transpose_a=True
    )
    columns = jnp.where(row_live[:, None], columns, 0.0)
    updated = jnp.where(row_live, residual_diag - jnp.sum(columns * columns, axis=1), residual_diag)
    columns, updated = (columns, updated)
    is_pivot = jnp.any(
        (local_row[:, None] == jnp.arange(total_rows)[None, :]) & is_owned[:, None], axis=0
    )
    updated = jnp.where(is_pivot, 0.0, updated)
    local_peak = jnp.max(jnp.where(row_live, updated, 0.0))
    peak = one_axis_at_a_time(local_peak, (("rows_0", "rows_1"), ("rows_2", "grp")))
    return (columns, updated / peak, peak)


def solution(mesh):
    split = Mesh(
        mesh.devices.reshape(8, 4, 2, mesh.shape["grp"]), ("rows_0", "rows_1", "rows_2", "grp")
    )
    in_specs = (P(ROWS_GRP, None), P(ROWS_GRP, None), P(ROWS_GRP), P(ROWS_GRP), P(ROWS_GRP), P())
    out_specs = (P(ROWS_GRP, None), P(ROWS_GRP), P())
    return jax.shard_map(
        on_device, mesh=split, in_specs=in_specs, out_specs=out_specs, check_vma=False
    )
```

profile of v0, /device:TPU:1, one launch (start us, length us, event | category | flops | bytes accessed | tf_op | source)
XLA Modules:
  0.0 141.8 jit_solution(15851015451289126972)
XLA Ops:
  0.6 0.7 and_select_fusion.1
  1.3 0.7 compare_reduce_fusion
  2.0 0.1 copy.40
  2.1 0.1 reduce-window.8
  2.2 0.1 fusion.19
  2.4 0.6 and_reduce_fusion
  3.0 0.6 select_reduce_fusion.2
  4.9 0.6 broadcast_in_dim.87
  5.5 12.0 %all-to-all-start = ((s32[32,1,1]{2,1,0:T(1,128)}), s32[32,1,1]{2,1,0:T(1,128)S(1)}, u32[]{:S(2)}, u32[]{:S(2)}) async-start(s32[32,1,1]{2,1,0:T(1,128)} %broadcast_in_dim.87), calls=%async_computation | async-start | bytes 32768 | tf_op jit(solution)/shard_map/all_to_all | solution.py:13
  17.6 1.3 fusion.22
  18.8 0.7 compare_select_fusion
  19.5 1.4 copy.42
  20.9 0.6 gather_fusion.1
  21.5 0.2 fusion.15
  21.7 5.5 %gather_fusion = bf16[64,2048]{1,0:T(8,128)(2,1)S(1)} fusion(bf16[2048,2048]{1,0:T(8,128)(2,1)} %param.6, s32[1024]{0:T(1024)S(1)} %pad_clamp_fusion), kind=kCustom, calls=%fused_computation | custom fusion | bytes 524544 | tf_op jit(solution)/shard_map/gather | solution.py:63
  27.2 0.2 fusion.6
  27.4 0.9 broadcast_in_dim.94
  28.3 9.2 %all-to-all-start.2 = ((f32[32,1,2112]{2,1,0:T(1,128)}), f32[32,1,2112]{2,1,0:T(1,128)S(1)}, u32[]{:S(2)}, u32[]{:S(2)}) async-start(f32[32,1,2112]{2,1,0:T(1,128)} %broadcast_in_dim.94), calls=%async_computation.2 | async-start | bytes 557056 | tf_op jit(solution)/shard_map/all_to_all | solution.py:13
  37.5 0.7 reduce.29
  38.2 10.1 %all-to-all-done.2 = f32[32,1,2112]{2,1,0:T(1,128)S(1)} async-done(((f32[32,1,2112]{2,1,0:T(1,128)}), f32[32,1,2112]{2,1,0:T(1,128)S(1)}, u32[]{:S(2)}, u32[]{:S(2)}) %all-to-all-start.2) | async-done | bytes 270368 | tf_op jit(solution)/shard_map/all_to_all | solution.py:13
  48.2 0.6 broadcast_in_dim.88
  48.8 7.7 %all-to-all-start.1 = ((s32[8,32,1]{1,2,0:T(1,128)}), s32[8,32,1]{1,2,0:T(1,128)S(1)}, u32[]{:S(2)}, u32[]{:S(2)}) async-start(s32[8,32,1]{1,2,0:T(1,128)} %broadcast_in_dim.88), calls=%async_computation.1 | async-start | bytes 8192 | tf_op jit(solution)/shard_map/all_to_all | solution.py:13
  56.6 4.5 %all-to-all-done.1 = s32[8,32,1]{1,2,0:T(1,128)S(1)} async-done(((s32[8,32,1]{1,2,0:T(1,128)}), s32[8,32,1]{1,2,0:T(1,128)S(1)}, u32[]{:S(2)}, u32[]{:S(2)}) %all-to-all-start.1) | async-done | bytes 1056 | tf_op jit(solution)/shard_map/all_to_all | solution.py:13
  61.1 1.5 %broadcast_in_dim.95 = f32[8,32,1,2112]{3,1,2,0:T(8,128)} broadcast(f32[32,2112]{1,0:T(8,128)S(1)} %bitcast.50), dimensions={1,3} | broadcast | bytes 2433024 | tf_op jit(solution)/shard_map/broadcast_in_dim | solution.py:12
  62.6 4.3 %all-to-all-start.3 = ((f32[8,32,1,2112]{3,1,2,0:T(8,128)}), f32[8,32,1,2112]{3,1,2,0:T(8,128)S(1)}, u32[]{:S(2)}, u32[]{:S(2)}) async-start(f32[8,32,1,2112]{3,1,2,0:T(8,128)} %broadcast_in_dim.95), calls=%async_computation.3 | async-start | bytes 4456448 | tf_op jit(solution)/shard_map/all_to_all | solution.py:13
  66.9 0.2 fusion.4
  67.2 0.1 copy.41
  67.3 0.1 eq.64
  67.4 27.2 %all-to-all-done.3 = f32[8,32,1,2112]{3,1,2,0:T(8,128)S(1)} async-done(((f32[8,32,1,2112]{3,1,2,0:T(8,128)}), f32[8,32,1,2112]{3,1,2,0:T(8,128)S(1)}, u32[]{:S(2)}, u32[]{:S(2)}) %all-to-all-start.3) | async-done | bytes 2162720 | tf_op jit(solution)/shard_map/all_to_all | solution.py:13
  94.5 1.3 copy.56
  95.9 0.9 fusion.1
  96.8 0.3 fusion.9
  97.1 6.1 %fusion = f32[2048,64]{0,1:T(8,128)S(1)} fusion(f32[2048,64]{0,1:T(8,128)S(1)} %copy-done, bf16[2048,2048]{1,0:T(8,128)(2,1)} %param.6, f32[64,2048]{1,0:T(8,128)S(1)} %fusion.1), kind=kOutput, calls=%fused_computation.3 | convolution fusion | flops 537133056 | bytes 9961472 | tf_op jit(solution)/shard_map/dot_general | solution.py:90
  103.1 0.6 convolution_subtract_fusion
  103.7 0.1 copy.46
  103.8 5.8 %cholesky.15 = f32[64,64]{1,0:T(8,128)S(1)} custom-call(f32[64,64]{1,0:T(8,128)S(1)} %fusion.14), custom_call_target="Cholesky" | custom-call | tf_op jit(solution)/shard_map/jit(cholesky)/cholesky | solution.py:87
  109.7 0.6 compare_reduce_fusion.1
  110.3 0.7 fusion.12
  111.0 4.9 %custom-call.6 = f32[1,64,64]{1,2,0:T(8,128)S(1)} custom-call(f32[1,64,64]{2,1,0:T(8,128)S(1)} %fusion.12), custom_call_target="InvertDiagBlocksLowerTriangular" | custom-call | tf_op jit(solution)/shard_map/triangular_solve | solution.py:93
  115.9 1.5 %multiply_reduce_fusion = (f32[2048]{0:T(1024)S(1)}, f32[2048,64]{0,1:T(8,128)}) fusion(f32[2048,64]{0,1:T(8,128)S(1)} %fusion, f32[1,64,64]{1,2,0:T(8,128)S(1)} %custom-call.6, pred[2048]{0:T(1024)(128)(4,1)S(1)} %broadcast_bitcast_fusion), kind=kOutput, calls=%fused_computation.9 | convolution fusion | flops 101054464 | bytes 1075200 | tf_op jit(solution)/shard_map/triangular_solve | solution.py:93
  117.3 0.7 select_reduce_fusion.1
  118.0 0.6 broadcast_in_dim.98
  118.7 7.8 %all_to_all.39 = f32[8,1,1]{2,1,0:T(1,128)S(1)} all-to-all(f32[8,1,1]{2,1,0:T(1,128)S(1)} %broadcast_in_dim.98), channel_id=1, replica_groups=mesh['rows_0'=8,'rows_1'=4,'rows_2'=2,'grp'=4] {'rows_2','grp'}, dimensions={0} | all-to-all | bytes 64 | tf_op jit(solution)/shard_map/all_to_all | solution.py:13
  126.5 0.6 reduce_max.28
  127.1 0.7 broadcast_in_dim.99
  127.7 12.1 %all_to_all.40 = f32[32,1,1]{2,1,0:T(1,128)S(1)} all-to-all(f32[32,1,1]{2,1,0:T(1,128)S(1)} %broadcast_in_dim.99), channel_id=1, replica_groups=mesh['rows_0'=8,'rows_1'=4,'rows_2'=2,'grp'=4] {'rows_0','rows_1'}, dimensions={0} | all-to-all | bytes 256 | tf_op jit(solution)/shard_map/all_to_all | solution.py:13
  139.8 0.6 reduce_max.29
  140.5 1.3 broadcast_divide_fusion
  (15 shorter events, 0.2 us)
Async XLA Ops:
  5.5 21.9 %all-to-all-start = ((s32[32,1,1]{2,1,0:T(1,128)}), s32[32,1,1]{2,1,0:T(1,128)S(1)}, u32[]{:S(2)}, u32[]{:S(2)}) async-start(s32[32,1,1]{2,1,0:T(1,128)} %broadcast_in_dim.87), calls=%async_computation | async-start | bytes 32768 | tf_op jit(solution)/shard_map/all_to_all | solution.py:13
  28.3 19.9 %all-to-all-start.2 = ((f32[32,1,2112]{2,1,0:T(1,128)}), f32[32,1,2112]{2,1,0:T(1,128)S(1)}, u32[]{:S(2)}, u32[]{:S(2)}) async-start(f32[32,1,2112]{2,1,0:T(1,128)} %broadcast_in_dim.94), calls=%async_computation.2 | async-start | bytes 557056 | tf_op jit(solution)/shard_map/all_to_all | solution.py:13
  48.8 12.2 %all-to-all-start.1 = ((s32[8,32,1]{1,2,0:T(1,128)}), s32[8,32,1]{1,2,0:T(1,128)S(1)}, u32[]{:S(2)}, u32[]{:S(2)}) async-start(s32[8,32,1]{1,2,0:T(1,128)} %broadcast_in_dim.88), calls=%async_computation.1 | async-start | bytes 8192 | tf_op jit(solution)/shard_map/all_to_all | solution.py:13
  62.6 4.5 %copy-start.2 = (s32[16]{0:T(128)S(1)}, s32[16]{0:T(128)}, u32[]{:S(2)}) copy-start(s32[16]{0:T(128)} %param.10) | copy-start | bytes 196
  62.6 32.0 %all-to-all-start.3 = ((f32[8,32,1,2112]{3,1,2,0:T(8,128)}), f32[8,32,1,2112]{3,1,2,0:T(8,128)S(1)}, u32[]{:S(2)}, u32[]{:S(2)}) async-start(f32[8,32,1,2112]{3,1,2,0:T(8,128)} %broadcast_in_dim.95), calls=%async_computation.3 | async-start | bytes 4456448 | tf_op jit(solution)/shard_map/all_to_all | solution.py:13
  95.8 1.2 copy-start
  103.1 14.2 %copy-start.1 = (f32[2048]{0:T(1024)S(1)}, f32[2048]{0:T(1024)}, u32[]{:S(2)}) copy-start(f32[2048]{0:T(1024)} %param.8) | copy-start | bytes 24580
where the time goes:
time: 142 us
  waiting for transfers between devices  41.7 us (29%)
  starting transfers between devices  33.3 us (23%)
  other arithmetic  21 us (15%)
  blocking collectives  19.9 us (14%)
  local copies, waits for them, and re-layouts  14.1 us (10%)
  matrix products  9.67 us (7%)
  between operations  2.09 us (1%)
    all_to_all x4, waiting for transfers between devices, copy_for_each(): return lax.all_to_all(copies, axis, split_axis=0, concat_axis=0, tiled=True)  41.7 us
    all_to_all x4, starting transfers between devices, copy_for_each(): return lax.all_to_all(copies, axis, split_axis=0, concat_axis=0, tiled=True)  33.3 us
    all_to_all x2, blocking collectives, copy_for_each(): return lax.all_to_all(copies, axis, split_axis=0, concat_axis=0, tiled=True)  19.9 us
    another operation x3, other arithmetic, on_device(): lower_factor = jnp.linalg.cholesky(pivot_block - gram)  6.52 us
    dot_general x1, matrix products, on_device(): jnp.dot(cholesky_vectors, picked.T, preferred_element_type=jnp.float32)  6.05 us
    another operation x2, other arithmetic, on_device(): lax.linalg.triangular_solve(lower_factor, remain, left_side=False, lower=...  5.55 us
    gather x1, local copies, waits for them, and re-layouts, on_device(): cholesky_vectors[local_row]  5.47 us
    broadcast_in_dim x6, local copies, waits for them, and re-layouts, copy_for_each(): copies = jnp.broadcast_to(value, (lax.axis_size(axis), *value.shape))  4.9 us
  transfers between devices with their start and end apart: 4, of which 3 were waited for; matrix products, arithmetic and copies ran while one was open for 8% of the time, Pallas kernels for 0%

commit v1 on v0

v1 whole, which is shorter than its diff:
```python
import jax
import jax.numpy as jnp
from jax import lax
from jax.experimental import pallas as pl
from jax.experimental.pallas import tpu as pltpu
from jax.sharding import Mesh
from jax.sharding import PartitionSpec as P

AXES = ("z", "y", "c", "x")
LANES = 128
LIVE_MOST = 12
VMEM = pl.BlockSpec(memory_space=pltpu.VMEM)
SMEM = pl.BlockSpec(memory_space=pltpu.SMEM)
ANY = pl.BlockSpec(memory_space=pltpu.HBM)
F32 = jnp.float32
BF16 = jnp.bfloat16


def iota(shape, dim):
    return lax.broadcasted_iota(jnp.int32, shape, dim)


def dot_lanes(a, b, **kw):
    return lax.dot_general(a, b, (((1,), (1,)), ((), ())), preferred_element_type=F32, **kw)


def dot(a, b):
    return lax.dot_general(a, b, (((1,), (0,)), ((), ())), preferred_element_type=F32)


def halves(a):
    hi = a.astype(BF16)
    return hi, (a - hi.astype(F32)).astype(BF16)


def pick_kernel(count, piv_ref, spb_ref, vec_ref, ict_ref, out_ref, meta_ref, vbuf, ibuf, sems):
    piv = piv_ref[...]
    group, offset = piv >> 7, piv & (LANES - 1)
    code = jnp.zeros(piv.shape, jnp.int32)
    for s in range(spb_ref.shape[0]):
        code = jnp.where(
            group == spb_ref[s], (s * LANES + offset) * count + iota(piv.shape, 1) + 1, code
        )
    best = jnp.max(code.astype(F32)).astype(jnp.int32)
    has = best > 0
    at = jnp.maximum(best - 1, 0)
    row, q = at // count, at % count
    vcopy = pltpu.make_async_copy(
        vec_ref.at[pl.ds(pl.multiple_of((row // 8) * 8, 8), 8), :], vbuf, sems.at[0]
    )
    icopy = pltpu.make_async_copy(
        ict_ref.at[:, pl.ds(pl.multiple_of((row // LANES) * LANES, LANES), LANES)],
        ibuf.at[pl.ds(count, count), :],
        sems.at[1],
    )
    vcopy.start()
    icopy.start()
    meta_ref[0] = jnp.where(has, row, -1)
    ibuf[pl.ds(0, count), :] = jnp.zeros((count, LANES), F32)
    k = vbuf.shape[1]
    vcopy.wait()
    mine = (iota(vbuf.shape, 0) == row % 8) & has
    vrow = jnp.sum(jnp.where(mine, vbuf[...].astype(F32), 0.0), axis=0, keepdims=True)
    out_ref[:, pl.ds(0, k)] = jnp.broadcast_to(vrow, (out_ref.shape[0], k))
    icopy.wait()
    tile = (out_ref.shape[0], LANES)
    hot = jnp.where((iota(tile, 1) == row % LANES) & has, 1.0, 0.0)
    ints = dot_lanes(hot, ibuf[...], precision=lax.Precision.HIGHEST)
    index = jnp.where(has, q + 1, 0).astype(F32)
    out_ref[:, pl.ds(k, LANES)] = jnp.where(iota(tile, 1) == 0, index, ints)


def pick(pivots, spb, vec, ict, copies):
    count, k = pivots.shape[1], vec.shape[1]
    return pl.pallas_call(
        lambda *refs: pick_kernel(count, *refs),
        out_shape=(
            jax.ShapeDtypeStruct((copies, k + LANES), F32),
            jax.ShapeDtypeStruct((1,), jnp.int32),
        ),
        in_specs=[VMEM, SMEM, ANY, ANY],
        out_specs=(VMEM, SMEM),
        scratch_shapes=[
            pltpu.VMEM((8, k), BF16),
            pltpu.VMEM((2 * count, LANES), F32),
            pltpu.SemaphoreType.DMA((2,)),
        ],
        compiler_params=pltpu.CompilerParams(vmem_limit_bytes=63 << 20),
        name="pick",
    )(pivots, spb, vec, ict)


def place_kernel(rows_ref, out_ref):
    k = rows_ref.shape[1] - LANES
    tail = rows_ref[:, pl.ds(k, LANES)]
    hot = tail[:, 0:1].astype(jnp.int32) - 1 == iota((rows_ref.shape[0], out_ref.shape[0]), 1)
    hot = jnp.where(hot, 1.0, 0.0).astype(BF16)
    turn = (((0,), (0,)), ((), ()))
    out_ref[:, pl.ds(0, k)] = lax.dot_general(
        hot, rows_ref[:, pl.ds(0, k)].astype(BF16), turn, preferred_element_type=F32
    )
    total = jnp.zeros((out_ref.shape[0], LANES), F32)
    for _ in range(3):
        part = tail.astype(BF16)
        tail = tail - part.astype(F32)
        total += lax.dot_general(hot, part, turn, preferred_element_type=F32)
    out_ref[:, pl.ds(k, LANES)] = total


def place(rows, count):
    return pl.pallas_call(
        place_kernel,
        out_shape=jax.ShapeDtypeStruct((count, rows.shape[1]), F32),
        in_specs=[VMEM],
        out_specs=VMEM,
        compiler_params=pltpu.CompilerParams(vmem_limit_bytes=8 << 20),
        name="place",
    )(rows)


def inverse_factor(m_ref, d_ref, count):
    for at in range(count):
        m = m_ref[...]
        row = m_ref[pl.ds(at, 1), :]
        d = row[:, count + at : count + at + 1]
        col = m[:, count + at : count + at + 1] / d
        below = iota((count, 1), 0) > at
        m_ref[...] = m - jnp.where(below, col, 0.0) * row
        d_ref[pl.ds(at, 1), :] = jnp.broadcast_to(d, (1, LANES))
    return m_ref[:, pl.ds(0, count)] * lax.rsqrt(d_ref[:, pl.ds(0, count)])


def step_kernel(
    here_ref, there_ref, vec_ref, ict_ref, diag_ref, live_ref, meta_ref,
    cols_ref, upd_ref, top_ref,
    vbuf, ibuf, dbuf, padded, m_ref, d_ref, remain, slots, vsems, sems,
):
    most, blk, k = vbuf.shape
    count = here_ref.shape[0]
    total = live_ref.shape[0]
    found = jnp.int32(0)
    for s in range(total):
        slots[found] = s
        found += live_ref[s]
    for s in range(total):
        slots[found] = s
        found += 1 - live_ref[s]
    vcopies = []
    for j in range(most):
        start = pl.multiple_of(slots[j] * blk, blk)
        vcopies.append(
            pltpu.make_async_copy(vec_ref.at[pl.ds(start, blk), :], vbuf.at[j], vsems.at[j])
        )
        vcopies[-1].start()
    icopy = pltpu.make_async_copy(ict_ref, ibuf, sems.at[0])
    icopy.start()
    dcopy = pltpu.make_async_copy(diag_ref, dbuf, sems.at[1])
    dcopy.start()

    cols_ref[...] = jnp.zeros(cols_ref.shape, F32)
    picked = (here_ref[:, pl.ds(0, k)] + there_ref[:, pl.ds(0, k)]).astype(BF16)
    padded[pl.ds(0, count), :] = jnp.zeros((count, k), BF16)
    padded[pl.ds(count, count), :] = picked
    ints = here_ref[:, pl.ds(k, LANES)] + there_ref[:, pl.ds(k, LANES)]
    schur = ints - dot_lanes(picked, padded[...])
    tile = (count, LANES)
    eye = jnp.where(iota(tile, 0) == iota(tile, 1), 1.0, 0.0)
    m_ref[...] = jnp.where(iota(tile, 1) < count, eye, schur)
    lower = halves(inverse_factor(m_ref, d_ref, count))

    icopy.wait()
    dcopy.wait()
    for j in range(most):
        vcopies[j].wait()
        prod = dot_lanes(vbuf[j], padded[...])
        start = pl.multiple_of(slots[j] * blk, blk)
        remain[:, pl.ds(j * blk, blk)] = ibuf[:, pl.ds(start, blk)] - prod.T[count:, :]
    upd_ref[...] = dbuf[...]
    high, low = halves(remain[...])
    cols = dot(lower[0], high) + dot(lower[0], low) + dot(lower[1], high)
    top = jnp.zeros((1, blk), F32)
    for j in range(most):
        s = slots[j]
        live = live_ref[s] > 0
        mine = cols[:, j * blk : (j + 1) * blk]
        left = dbuf[pl.ds(s, 1), :] - jnp.sum(mine * mine, axis=0, keepdims=True)
        left = jnp.where(iota((1, blk), 1) + s * blk == meta_ref[0], 0.0, left)
        cols_ref[:, pl.ds(pl.multiple_of(s * blk, blk), blk)] = jnp.where(live, mine, 0.0)
        upd_ref[pl.ds(s, 1), :] = jnp.where(live, left, dbuf[pl.ds(s, 1), :])
        top = jnp.maximum(top, jnp.where(live, left, 0.0))
    top_ref[...] = jnp.broadcast_to(top, top_ref.shape)


def step(here, there, vec, ict, diag, live, meta, copies):
    count, rows = ict.shape
    k = vec.shape[1]
    total = live.shape[0]
    blk = rows // total
    most = min(LIVE_MOST, total)
    return pl.pallas_call(
        step_kernel,
        out_shape=(
            jax.ShapeDtypeStruct((count, rows), F32),
            jax.ShapeDtypeStruct((total, blk), F32),
            jax.ShapeDtypeStruct((copies, blk), F32),
        ),
        in_specs=[VMEM, VMEM, ANY, ANY, ANY, SMEM, SMEM],
        out_specs=(VMEM, VMEM, VMEM),
        scratch_shapes=[
            pltpu.VMEM((most, blk, k), BF16),
            pltpu.VMEM((count, rows), F32),
            pltpu.VMEM((total, blk), F32),
            pltpu.VMEM((2 * count, k), BF16),
            pltpu.VMEM((count, LANES), F32),
            pltpu.VMEM((count, LANES), F32),
            pltpu.VMEM((count, most * blk), F32),
            pltpu.SMEM((total + 1,), jnp.int32),
            pltpu.SemaphoreType.DMA((most,)),
            pltpu.SemaphoreType.DMA((2,)),
        ],
        compiler_params=pltpu.CompilerParams(vmem_limit_bytes=24 << 20),
        name="step",
    )(here, there, vec, ict, diag, live, meta)


def scale_kernel(tops_ref, upd_ref, rel_ref, peak_ref):
    peak = jnp.max(jnp.max(tops_ref[...], axis=0, keepdims=True), axis=1, keepdims=True)
    rel_ref[...] = upd_ref[...] / peak
    peak_ref[...] = peak


def scale(tops, upd):
    return pl.pallas_call(
        scale_kernel,
        out_shape=(
            jax.ShapeDtypeStruct(upd.shape, F32),
            jax.ShapeDtypeStruct((1, 1), F32),
        ),
        in_specs=[VMEM, VMEM],
        out_specs=(VMEM, VMEM),
        compiler_params=pltpu.CompilerParams(vmem_limit_bytes=4 << 20),
        name="scale",
    )(tops, upd)


def exchange(blocks, axes):
    return lax.all_to_all(blocks, axes, split_axis=0, concat_axis=0, tiled=True)


def on_device(vec, ints, diag, spb, live, pivots):
    count = pivots.shape[0]
    ict = ints.T
    sizes = {a: lax.axis_size(a) for a in AXES}
    near = sizes["y"] * sizes["x"]
    mine, meta = pick(pivots[None, :], spb, vec, ict, sizes["z"])
    column = exchange(mine, "z")
    rows = exchange(jnp.broadcast_to(column, (near, *column.shape)), ("y", "x"))
    placed = place(rows.reshape(-1, rows.shape[-1]), count)
    other = lax.ppermute(placed, "c", [(0, 1), (1, 0)])
    cols, upd, top = step(
        placed, other, vec, ict, diag.reshape(live.shape[0], -1), live, meta, near * sizes["z"] * sizes["c"]
    )
    rel, peak = scale(exchange(top, AXES), upd)
    return (cols.T, rel.reshape(-1), peak.reshape(()))


def solution(mesh):
    split = Mesh(mesh.devices.reshape(8, 4, 2, mesh.shape["grp"]), AXES)
    in_specs = (P(AXES, None), P(AXES, None), P(AXES), P(AXES), P(AXES), P())
    out_specs = (P(AXES, None), P(AXES), P())
    return jax.shard_map(
        on_device, mesh=split, in_specs=in_specs, out_specs=out_specs, check_vma=False
    )
```

time: 142 us -> 85.4 us (0.60)
  waiting for transfers between devices: 41.7 us -> 1.58 us
  blocking collectives: 19.9 us -> 56.8 us
  starting transfers between devices: 33.3 us -> 3.23 us
  other arithmetic: 21 us -> 0 us
  Pallas kernels: 0 us -> 18.3 us
  local copies, waits for them, and re-layouts: 14.1 us -> 4.42 us
  matrix products: 9.67 us -> 0 us
  between operations: 2.09 us -> 0.67 us
    all_to_all x4 -> x0, waiting for transfers between devices: 41.7 us -> none  [copy_for_each(): return lax.all_to_all(copies, axis, split_axis=0, concat_axis=0, tiled=True)]
    all_to_all x2 -> x3, blocking collectives: 19.9 us -> 56.8 us  [exchange(): return lax.all_to_all(blocks, axes, split_axis=0, concat_axis=0, tiled=True)]
    all_to_all x4 -> x0, starting transfers between devices: 33.3 us -> none  [copy_for_each(): return lax.all_to_all(copies, axis, split_axis=0, concat_axis=0, tiled=True)]
    pallas_call x0 -> x4, Pallas kernels: none -> 18.3 us  [the longest x1 14.6 us: step(): pl.pallas_call(step_kernel, out_shape=(jax.ShapeDtypeStruct((count, rows)...]
    another operation x7 -> x0, other arithmetic: 13.4 us -> none  [the longest x3 6.52 us: on_device(): lower_factor = jnp.linalg.cholesky(pivot_block - gram)]
    dot_general x6 -> x0, matrix products: 8.22 us -> none  [the longest x1 6.05 us: on_device(): jnp.dot(cholesky_vectors, picked.T, preferred_element_type=jnp.float32)]
    gather x2 -> x0, local copies, waits for them, and re-layouts: 6.07 us -> none  [the longest x1 5.47 us: on_device(): cholesky_vectors[local_row]]
    broadcast_in_dim x6 -> x1, local copies, waits for them, and re-layouts: 4.9 us -> 0.07 us  [on_device(): rows = exchange(jnp.broadcast_to(column, (near, *column.shape)), ('y', 'x'))]
  transfers between devices with their start and end apart: 4 -> 1, of which waited for: 3 -> 1; matrix products, arithmetic and copies ran while one was open for 8% -> 0% of each run, Pallas kernels for 0% -> 0%
where the time goes in v1:
time: 85.4 us; the launch traced here: 85 us
  blocking collectives  56.8 us (67%)
  Pallas kernels  18.3 us (21%)
  local copies, waits for them, and re-layouts  4.42 us (5%)
  starting transfers between devices  3.23 us (4%)
  waiting for transfers between devices  1.58 us (2%)
    all_to_all x3, blocking collectives, exchange(): return lax.all_to_all(blocks, axes, split_axis=0, concat_axis=0, tiled=True)  56.8 us
    pallas_call x1, Pallas kernels, step(): pl.pallas_call(step_kernel, out_shape=(jax.ShapeDtypeStruct((count, rows)...  14.6 us
    unnamed x9, local copies, waits for them, and re-layouts  3.39 us
    ppermute x1, starting transfers between devices, on_device(): other = lax.ppermute(placed, 'c', [(0, 1), (1, 0)])  3.23 us
    pallas_call x1, Pallas kernels, pick(): pl.pallas_call(lambda *refs: pick_kernel(count, *refs), out_shape=(jax.Sh...  2.6 us
  transfers between devices with their start and end apart: 1, of which 1 were waited for; matrix products, arithmetic and copies ran while one was open for 0% of the time, Pallas kernels for 0%

profile of v1, /device:TPU:1, one launch (start us, length us, event | category | flops | bytes accessed | tf_op | source)
XLA Modules:
  0.0 85.0 jit_solution(15155621226926210842)
XLA Ops:
  0.6 2.6 %pick.1 = (f32[8,2176]{1,0:T(8,128)}, s32[1]{0:T(128)}) custom-call(s32[1,64]{1,0:T(1,128)} %bitcast.23, s32[16]{0:T(128)} %refs_1_.1, bf16[2048,2048]{1,0:T(8,128)(2,1)} %vec_ref.1, f32[64,2048]{1,0:T(8,128)} %bitcast.16), custom_call_target="tpu_custom_call" | custom-call | tf_op jit(solution)/shard_map/pick/pallas_call | solution.py:75
  3.2 1.0 %copy.9 = f32[8,1,2176]{2,1,0:T(1,128)S(1)} copy(f32[8,1,2176]{2,0,1:T(8,128)} %bitcast.22) | data formatting | bytes 139264 | tf_op jit(solution)/shard_map/all_to_all | solution.py:247
  4.2 16.2 %all_to_all.28 = f32[8,1,2176]{2,1,0:T(1,128)S(1)} all-to-all(f32[8,1,2176]{2,1,0:T(1,128)S(1)} %copy.9), channel_id=1, replica_groups=mesh['z'=8,'y'=4,'c'=2,'x'=4] {'z'}, dimensions={0} | all-to-all | bytes 139264 | tf_op jit(solution)/shard_map/all_to_all | solution.py:247
  20.4 0.1 broadcast_in_dim.7
  20.5 22.6 %all_to_all.29 = f32[16,8,2176]{2,1,0:T(8,128)S(1)} all-to-all(f32[16,8,2176]{2,1,0:T(8,128)S(1)} %broadcast_in_dim.7), channel_id=1, replica_groups=mesh['z'=8,'y'=4,'c'=2,'x'=4] {'y','x'}, dimensions={0} | all-to-all | bytes 2228224 | tf_op jit(solution)/shard_map/all_to_all | solution.py:247
  43.1 0.0 copy-start.1
  43.1 0.0 copy-start.2
  43.1 0.0 copy-start.3
  43.1 0.4 place.1.here_ref
  43.5 3.2 %collective-permute-start = (f32[64,2176]{1,0:T(8,128)S(1)}, f32[64,2176]{1,0:T(8,128)S(1)}, u32[]{:S(2)}, u32[]{:S(2)}) collective-permute-start(f32[64,2176]{1,0:T(8,128)S(1)} %place.1.here_ref), channel_id=1, source_target_pairs={{0,4},{4,0},{1,5},{5,1},{2,6},{6,2},{3,7},{7,3},{8,12},{12,8},{9,1... | collective-permute-start | bytes 1671176 | tf_op jit(solution)/shard_map/ppermute | solution.py:259
  46.7 1.6 %collective-permute-done.there_ref = f32[64,2176]{1,0:T(8,128)S(1)} collective-permute-done((f32[64,2176]{1,0:T(8,128)S(1)}, f32[64,2176]{1,0:T(8,128)S(1)}, u32[]{:S(2)}, u32[]{:S(2)}) %collective-permute-start) | collective-permute-done | bytes 557088 | tf_op jit(solution)/shard_map/ppermute | solution.py:259
  48.3 0.0 copy-done.1
  48.3 0.0 copy-done.2
  48.3 0.0 copy-done.3
  48.3 0.0 copy-start
  48.3 3.4 %copy-done = bf16[2048,2048]{1,0:T(8,128)(2,1)S(1)} copy-done((bf16[2048,2048]{1,0:T(8,128)(2,1)S(1)}, bf16[2048,2048]{1,0:T(8,128)(2,1)}, u32[]{:S(2)}) %copy-start) | copy-done | bytes 8388632
  51.7 14.6 %step.1 = (f32[64,2048]{1,0:T(8,128)}, f32[16,128]{1,0:T(8,128)S(1)}, f32[256,128]{1,0:T(8,128)S(1)}) custom-call(f32[64,2176]{1,0:T(8,128)S(1)} %place.1.here_ref, f32[64,2176]{1,0:T(8,128)S(1)} %collective-permute-done.there_ref, bf16[2048,2048]{1,0:T(8,128)(2,1)S(1)} %copy-done, f32[64,2048]{1,0:T(8,128)S(1)} %bitcast.17, f32[16,128]{1,0:T(8,128)S(1)} %bitcast.20, ...), custom_call_target="tpu_custom_call" | custom-call | tf_op jit(solution)/shard_map/step/pallas_call | solution.py:200
  66.3 18.0 %all_to_all.30 = f32[256,1,128]{2,1,0:T(1,128)S(1)} all-to-all(f32[256,1,128]{2,1,0:T(1,128)S(1)} %bitcast.19), channel_id=1, replica_groups=mesh['z'=8,'y'=4,'c'=2,'x'=4] {'z','y','c','x'}, dimensions={0} | all-to-all | bytes 262144 | tf_op jit(solution)/shard_map/all_to_all | solution.py:247
  84.3 0.7 scale.1
  (1 shorter events, 0.0 us)
Async XLA Ops:
  43.1 5.2 %copy-start.1 = (f32[2048,64]{0,1:T(8,128)S(1)}, f32[2048,64]{0,1:T(8,128)}, u32[]{:S(2)}) copy-start(f32[2048,64]{0,1:T(8,128)} %param.7) | copy-start | bytes 1572868
  43.1 5.2 %copy-start.2 = (f32[2048]{0:T(1024)S(1)}, f32[2048]{0:T(1024)}, u32[]{:S(2)}) copy-start(f32[2048]{0:T(1024)} %param.8) | copy-start | bytes 24580
  43.1 5.2 %copy-start.3 = (s32[16]{0:T(128)S(1)}, s32[16]{0:T(128)}, u32[]{:S(2)}) copy-start(s32[16]{0:T(128)} %live_ref.1) | copy-start | bytes 196
  43.5 4.8 %collective-permute-start = (f32[64,2176]{1,0:T(8,128)S(1)}, f32[64,2176]{1,0:T(8,128)S(1)}, u32[]{:S(2)}, u32[]{:S(2)}) collective-permute-start(f32[64,2176]{1,0:T(8,128)S(1)} %place.1.here_ref), channel_id=1, source_target_pairs={{0,4},{4,0},{1,5},{5,1},{2,6},{6,2},{3,7},{7,3},{8,12},{12,8},{9,1... | collective-permute-start | bytes 1671176 | tf_op jit(solution)/shard_map/ppermute | solution.py:259
  48.3 3.4 %copy-start = (bf16[2048,2048]{1,0:T(8,128)(2,1)S(1)}, bf16[2048,2048]{1,0:T(8,128)(2,1)}, u32[]{:S(2)}) copy-start(bf16[2048,2048]{1,0:T(8,128)(2,1)} %vec_ref.1) | copy-start | bytes 25165828

commit v2 on v1

--- a/solution.py
+++ b/solution.py
@@ -18,6 +18,10 @@
 
 def iota(shape, dim):
     return lax.broadcasted_iota(jnp.int32, shape, dim)
+
+
+def in_hbm(a):
+    return pltpu.with_memory_space_constraint(a, pltpu.HBM)
 
 
 def dot_lanes(a, b, **kw):
@@ -61,13 +65,17 @@
     vcopy.wait()
     mine = (iota(vbuf.shape, 0) == row % 8) & has
     vrow = jnp.sum(jnp.where(mine, vbuf[...].astype(F32), 0.0), axis=0, keepdims=True)
-    out_ref[:, pl.ds(0, k)] = jnp.broadcast_to(vrow, (out_ref.shape[0], k))
+    copies = out_ref.shape[0]
+    for i in range(copies):
+        out_ref[i, :, pl.ds(0, k)] = vrow
     icopy.wait()
-    tile = (out_ref.shape[0], LANES)
+    tile = (8, LANES)
     hot = jnp.where((iota(tile, 1) == row % LANES) & has, 1.0, 0.0)
     ints = dot_lanes(hot, ibuf[...], precision=lax.Precision.HIGHEST)
     index = jnp.where(has, q + 1, 0).astype(F32)
-    out_ref[:, pl.ds(k, LANES)] = jnp.where(iota(tile, 1) == 0, index, ints)
+    tail = jnp.where(iota(tile, 1) == 0, index, ints)[0:1]
+    for i in range(copies):
+        out_ref[i, :, pl.ds(k, LANES)] = tail
 
 
 def pick(pivots, spb, vec, ict, copies):
@@ -75,7 +83,7 @@
     return pl.pallas_call(
         lambda *refs: pick_kernel(count, *refs),
         out_shape=(
-            jax.ShapeDtypeStruct((copies, k + LANES), F32),
+            jax.ShapeDtypeStruct((copies, 1, k + LANES), F32),
             jax.ShapeDtypeStruct((1,), jnp.int32),
         ),
         in_specs=[VMEM, SMEM, ANY, ANY],
@@ -85,9 +93,9 @@
             pltpu.VMEM((2 * count, LANES), F32),
             pltpu.SemaphoreType.DMA((2,)),
         ],
-        compiler_params=pltpu.CompilerParams(vmem_limit_bytes=63 << 20),
+        compiler_params=pltpu.CompilerParams(vmem_limit_bytes=8 << 20),
         name="pick",
-    )(pivots, spb, vec, ict)
+    )(in_hbm(pivots), in_hbm(spb), in_hbm(vec), in_hbm(ict))
 
 
 def place_kernel(rows_ref, out_ref):
@@ -118,22 +126,35 @@
     )(rows)
 
 
-def inverse_factor(m_ref, d_ref, count):
-    for at in range(count):
-        m = m_ref[...]
-        row = m_ref[pl.ds(at, 1), :]
-        d = row[:, count + at : count + at + 1]
-        col = m[:, count + at : count + at + 1] / d
-        below = iota((count, 1), 0) > at
-        m_ref[...] = m - jnp.where(below, col, 0.0) * row
-        d_ref[pl.ds(at, 1), :] = jnp.broadcast_to(d, (1, LANES))
-    return m_ref[:, pl.ds(0, count)] * lax.rsqrt(d_ref[:, pl.ds(0, count)])
+def eliminate(blocks, at):
+    n = len(blocks)
+    lead = 8 * n + 8 * at
+    tile = blocks[0].shape
+    columns = [
+        {i: jnp.broadcast_to(blocks[i][:, lead + j : lead + j + 1], tile) for i in range(at, n)}
+        for j in range(8)
+    ]
+    pivot = jnp.ones(tile, F32)
+    for j in range(8):
+        row = jnp.broadcast_to(blocks[at][j : j + 1], tile)
+        d = jnp.broadcast_to(columns[j][at][j : j + 1], tile)
+        inverse = 1.0 / d
+        pivot = jnp.where(iota(tile, 0) == j, d, pivot)
+        across = [jnp.broadcast_to(columns[m][at][j : j + 1], tile) for m in range(j + 1, 8)]
+        for i in range(at, n):
+            by = columns[j][i] * inverse
+            if i == at:
+                by = jnp.where(iota(tile, 0) > j, by, 0.0)
+            blocks[i] = blocks[i] - by * row
+            for m in range(j + 1, 8):
+                columns[m][i] = columns[m][i] - by * across[m - j - 1]
+    return blocks[at] * lax.rsqrt(pivot)
 
 
 def step_kernel(
     here_ref, there_ref, vec_ref, ict_ref, diag_ref, live_ref, meta_ref,
     cols_ref, upd_ref, top_ref,
-    vbuf, ibuf, dbuf, padded, m_ref, d_ref, remain, slots, vsems, sems,
+    vbuf, padded, lower, remain, slots, vsems,
 ):
     most, blk, k = vbuf.shape
     count = here_ref.shape[0]
@@ -152,10 +173,6 @@
             pltpu.make_async_copy(vec_ref.at[pl.ds(start, blk), :], vbuf.at[j], vsems.at[j])
         )
         vcopies[-1].start()
-    icopy = pltpu.make_async_copy(ict_ref, ibuf, sems.at[0])
-    icopy.start()
-    dcopy = pltpu.make_async_copy(diag_ref, dbuf, sems.at[1])
-    dcopy.start()
 
     cols_ref[...] = jnp.zeros(cols_ref.shape, F32)
     picked = (here_ref[:, pl.ds(0, k)] + there_ref[:, pl.ds(0, k)]).astype(BF16)
@@ -165,28 +182,29 @@
     schur = ints - dot_lanes(picked, padded[...])
     tile = (count, LANES)
     eye = jnp.where(iota(tile, 0) == iota(tile, 1), 1.0, 0.0)
-    m_ref[...] = jnp.where(iota(tile, 1) < count, eye, schur)
-    lower = halves(inverse_factor(m_ref, d_ref, count))
-
-    icopy.wait()
-    dcopy.wait()
-    for j in range(most):
-        vcopies[j].wait()
-        prod = dot_lanes(vbuf[j], padded[...])
-        start = pl.multiple_of(slots[j] * blk, blk)
-        remain[:, pl.ds(j * blk, blk)] = ibuf[:, pl.ds(start, blk)] - prod.T[count:, :]
-    upd_ref[...] = dbuf[...]
+    whole = jnp.where(iota(tile, 1) < count, eye, schur)
+    panels = count // 8
+    blocks = [whole[8 * i : 8 * i + 8] for i in range(panels)]
+    for at in range(panels):
+        for j in range(most * at // panels, most * (at + 1) // panels):
+            vcopies[j].wait()
+            prod = dot_lanes(vbuf[j], padded[...])
+            start = pl.multiple_of(slots[j] * blk, blk)
+            remain[:, pl.ds(j * blk, blk)] = ict_ref[:, pl.ds(start, blk)] - prod.T[count:, :]
+        lower[pl.ds(8 * at, 8), :] = eliminate(blocks, at)
+    upd_ref[...] = diag_ref[...]
     high, low = halves(remain[...])
-    cols = dot(lower[0], high) + dot(lower[0], low) + dot(lower[1], high)
+    lhigh, llow = halves(lower[:, pl.ds(0, count)])
+    cols = dot(lhigh, high) + dot(lhigh, low) + dot(llow, high)
     top = jnp.zeros((1, blk), F32)
     for j in range(most):
         s = slots[j]
         live = live_ref[s] > 0
         mine = cols[:, j * blk : (j + 1) * blk]
-        left = dbuf[pl.ds(s, 1), :] - jnp.sum(mine * mine, axis=0, keepdims=True)
+        left = diag_ref[pl.ds(s, 1), :] - jnp.sum(mine * mine, axis=0, keepdims=True)
         left = jnp.where(iota((1, blk), 1) + s * blk == meta_ref[0], 0.0, left)
         cols_ref[:, pl.ds(pl.multiple_of(s * blk, blk), blk)] = jnp.where(live, mine, 0.0)
-        upd_ref[pl.ds(s, 1), :] = jnp.where(live, left, dbuf[pl.ds(s, 1), :])
+        upd_ref[pl.ds(s, 1), :] = jnp.where(live, left, diag_ref[pl.ds(s, 1), :])
         top = jnp.maximum(top, jnp.where(live, left, 0.0))
     top_ref[...] = jnp.broadcast_to(top, top_ref.shape)
 
@@ -204,23 +222,19 @@
             jax.ShapeDtypeStruct((total, blk), F32),
             jax.ShapeDtypeStruct((copies, blk), F32),
         ),
-        in_specs=[VMEM, VMEM, ANY, ANY, ANY, SMEM, SMEM],
+        in_specs=[VMEM, VMEM, ANY, VMEM, VMEM, SMEM, SMEM],
         out_specs=(VMEM, VMEM, VMEM),
         scratch_shapes=[
             pltpu.VMEM((most, blk, k), BF16),
-            pltpu.VMEM((count, rows), F32),
-            pltpu.VMEM((total, blk), F32),
             pltpu.VMEM((2 * count, k), BF16),
-            pltpu.VMEM((count, LANES), F32),
             pltpu.VMEM((count, LANES), F32),
             pltpu.VMEM((count, most * blk), F32),
             pltpu.SMEM((total + 1,), jnp.int32),
             pltpu.SemaphoreType.DMA((most,)),
-            pltpu.SemaphoreType.DMA((2,)),
         ],
         compiler_params=pltpu.CompilerParams(vmem_limit_bytes=24 << 20),
         name="step",
-    )(here, there, vec, ict, diag, live, meta)
+    )(here, there, in_hbm(vec), ict, diag, live, meta)
 
 
 def scale_kernel(tops_ref, upd_ref, rel_ref, peak_ref):
@@ -254,6 +268,7 @@
     near = sizes["y"] * sizes["x"]
     mine, meta = pick(pivots[None, :], spb, vec, ict, sizes["z"])
     column = exchange(mine, "z")
+    column = column.reshape(column.shape[0], -1)
     rows = exchange(jnp.broadcast_to(column, (near, *column.shape)), ("y", "x"))
     placed = place(rows.reshape(-1, rows.shape[-1]), count)
     other = lax.ppermute(placed, "c", [(0, 1), (1, 0)])

time: 85.4 us -> 75.9 us (0.89)
  Pallas kernels: 18.3 us -> 13.2 us
  local copies, waits for them, and re-layouts: 4.42 us -> 0.09 us
    pallas_call x1, Pallas kernels: 14.6 us -> 9.9 us  [step(): pl.pallas_call(step_kernel, out_shape=(jax.ShapeDtypeStruct((count, rows)...]
    unnamed x9 -> x7, local copies, waits for them, and re-layouts: 3.39 us -> 0.02 us
    all_to_all x1 -> x0, local copies, waits for them, and re-layouts: 0.96 us -> none  [exchange(): return lax.all_to_all(blocks, axes, split_axis=0, concat_axis=0, tiled=True)]
where the time goes in v2:
time: 75.9 us; the launch traced here: 75.6 us
  blocking collectives  56.8 us (75%)
  Pallas kernels  13.2 us (17%)
  starting transfers between devices  3.23 us (4%)
  waiting for transfers between devices  1.58 us (2%)
    all_to_all x3, blocking collectives, exchange(): return lax.all_to_all(blocks, axes, split_axis=0, concat_axis=0, tiled=True)  56.8 us
    pallas_call x1, Pallas kernels, step(): pl.pallas_call(step_kernel, out_shape=(jax.ShapeDtypeStruct((count, rows)...  9.9 us
    ppermute x1, starting transfers between devices, on_device(): other = lax.ppermute(placed, 'c', [(0, 1), (1, 0)])  3.23 us
    pallas_call x1, Pallas kernels, pick(): pl.pallas_call(lambda *refs: pick_kernel(count, *refs), out_shape=(jax.Sh...  2.27 us
    ppermute x1, waiting for transfers between devices, on_device(): other = lax.ppermute(placed, 'c', [(0, 1), (1, 0)])  1.58 us
  transfers between devices with their start and end apart: 1, of which 1 were waited for; matrix products, arithmetic and copies ran while one was open for 0% of the time, Pallas kernels for 0%

profile of v2, /device:TPU:1, one launch (start us, length us, event | category | flops | bytes accessed | tf_op | source)
XLA Modules:
  0.0 75.6 jit_solution(13507620930278278142)
XLA Ops:
  0.6 2.3 %pick.1 = (f32[8,1,2176]{2,1,0:T(1,128)S(1)}, s32[1]{0:T(128)}) custom-call(s32[1,64]{1,0:T(1,128)} %bitcast.21, s32[16]{0:T(128)} %refs_1_.1, bf16[2048,2048]{1,0:T(8,128)(2,1)} %vec_ref.1, f32[64,2048]{1,0:T(8,128)} %bitcast.15), custom_call_target="tpu_custom_call" | custom-call | tf_op jit(solution)/shard_map/pick/pallas_call | solution.py:83
  2.9 16.2 %all_to_all.21 = f32[8,1,2176]{2,1,0:T(1,128)S(1)} all-to-all(f32[8,1,2176]{2,1,0:T(1,128)S(1)} %get-tuple-element.10), channel_id=1, replica_groups=mesh['z'=8,'y'=4,'c'=2,'x'=4] {'z'}, dimensions={0} | all-to-all | bytes 139264 | tf_op jit(solution)/shard_map/all_to_all | solution.py:261
  19.1 0.1 broadcast_in_dim.7
  19.2 22.6 %all_to_all.22 = f32[16,8,2176]{2,1,0:T(8,128)S(1)} all-to-all(f32[16,8,2176]{2,1,0:T(8,128)S(1)} %broadcast_in_dim.7), channel_id=1, replica_groups=mesh['z'=8,'y'=4,'c'=2,'x'=4] {'y','x'}, dimensions={0} | all-to-all | bytes 2228224 | tf_op jit(solution)/shard_map/all_to_all | solution.py:261
  41.8 0.0 copy-start
  41.8 0.0 copy-start.1
  41.8 0.0 copy-start.2
  41.8 0.4 place.1.here_ref
  42.2 3.2 %collective-permute-start = (f32[64,2176]{1,0:T(8,128)S(1)}, f32[64,2176]{1,0:T(8,128)S(1)}, u32[]{:S(2)}, u32[]{:S(2)}) collective-permute-start(f32[64,2176]{1,0:T(8,128)S(1)} %place.1.here_ref), channel_id=1, source_target_pairs={{0,4},{4,0},{1,5},{5,1},{2,6},{6,2},{3,7},{7,3},{8,12},{12,8},{9,1... | collective-permute-start | bytes 1671176 | tf_op jit(solution)/shard_map/ppermute | solution.py:274
  45.4 1.6 %collective-permute-done.there_ref = f32[64,2176]{1,0:T(8,128)S(1)} collective-permute-done((f32[64,2176]{1,0:T(8,128)S(1)}, f32[64,2176]{1,0:T(8,128)S(1)}, u32[]{:S(2)}, u32[]{:S(2)}) %collective-permute-start) | collective-permute-done | bytes 557088 | tf_op jit(solution)/shard_map/ppermute | solution.py:274
  47.0 0.0 copy-done
  47.0 0.0 copy-done.1
  47.0 0.0 copy-done.2
  47.0 9.9 %step.1 = (f32[64,2048]{1,0:T(8,128)}, f32[16,128]{1,0:T(8,128)S(1)}, f32[256,128]{1,0:T(8,128)S(1)}) custom-call(f32[64,2176]{1,0:T(8,128)S(1)} %place.1.here_ref, f32[64,2176]{1,0:T(8,128)S(1)} %collective-permute-done.there_ref, bf16[2048,2048]{1,0:T(8,128)(2,1)} %vec_ref.1, f32[64,2048]{1,0:T(8,128)S(1)} %bitcast.16, f32[16,128]{1,0:T(8,128)S(1)} %bitcast.19, ...), custom_call_target="tpu_custom_call" | custom-call | tf_op jit(solution)/shard_map/step/pallas_call | solution.py:218
  56.9 18.0 %all_to_all.23 = f32[256,1,128]{2,1,0:T(1,128)S(1)} all-to-all(f32[256,1,128]{2,1,0:T(1,128)S(1)} %bitcast.18), channel_id=1, replica_groups=mesh['z'=8,'y'=4,'c'=2,'x'=4] {'z','y','c','x'}, dimensions={0} | all-to-all | bytes 262144 | tf_op jit(solution)/shard_map/all_to_all | solution.py:261
  74.9 0.7 scale.1
  (1 shorter events, 0.0 us)
Async XLA Ops:
  41.8 5.2 %copy-start = (f32[2048,64]{0,1:T(8,128)S(1)}, f32[2048,64]{0,1:T(8,128)}, u32[]{:S(2)}) copy-start(f32[2048,64]{0,1:T(8,128)} %param.7) | copy-start | bytes 1572868
  41.8 5.2 %copy-start.1 = (f32[2048]{0:T(1024)S(1)}, f32[2048]{0:T(1024)}, u32[]{:S(2)}) copy-start(f32[2048]{0:T(1024)} %param.8) | copy-start | bytes 24580
  41.8 5.2 %copy-start.2 = (s32[16]{0:T(128)S(1)}, s32[16]{0:T(128)}, u32[]{:S(2)}) copy-start(s32[16]{0:T(128)} %live_ref.1) | copy-start | bytes 196
  42.2 4.8 %collective-permute-start = (f32[64,2176]{1,0:T(8,128)S(1)}, f32[64,2176]{1,0:T(8,128)S(1)}, u32[]{:S(2)}, u32[]{:S(2)}) collective-permute-start(f32[64,2176]{1,0:T(8,128)S(1)} %place.1.here_ref), channel_id=1, source_target_pairs={{0,4},{4,0},{1,5},{5,1},{2,6},{6,2},{3,7},{7,3},{8,12},{12,8},{9,1... | collective-permute-start | bytes 1671176 | tf_op jit(solution)/shard_map/ppermute | solution.py:274

commit v3 on v2

--- a/solution.py
+++ b/solution.py
@@ -154,11 +154,12 @@
 def step_kernel(
     here_ref, there_ref, vec_ref, ict_ref, diag_ref, live_ref, meta_ref,
     cols_ref, upd_ref, top_ref,
-    vbuf, padded, lower, remain, slots, vsems,
+    padded, lower, remain, slots,
 ):
-    most, blk, k = vbuf.shape
-    count = here_ref.shape[0]
-    total = live_ref.shape[0]
+    count, total = here_ref.shape[0], live_ref.shape[0]
+    k = vec_ref.shape[1]
+    blk = vec_ref.shape[0] // total
+    most = remain.shape[1] // blk
     found = jnp.int32(0)
     for s in range(total):
         slots[found] = s
@@ -166,14 +167,6 @@
     for s in range(total):
         slots[found] = s
         found += 1 - live_ref[s]
-    vcopies = []
-    for j in range(most):
-        start = pl.multiple_of(slots[j] * blk, blk)
-        vcopies.append(
-            pltpu.make_async_copy(vec_ref.at[pl.ds(start, blk), :], vbuf.at[j], vsems.at[j])
-        )
-        vcopies[-1].start()
-
     cols_ref[...] = jnp.zeros(cols_ref.shape, F32)
     picked = (here_ref[:, pl.ds(0, k)] + there_ref[:, pl.ds(0, k)]).astype(BF16)
     padded[pl.ds(0, count), :] = jnp.zeros((count, k), BF16)
@@ -185,12 +178,17 @@
     whole = jnp.where(iota(tile, 1) < count, eye, schur)
     panels = count // 8
     blocks = [whole[8 * i : 8 * i + 8] for i in range(panels)]
+    chunk = 4
+    places = [1, 3, 5]
     for at in range(panels):
-        for j in range(most * at // panels, most * (at + 1) // panels):
-            vcopies[j].wait()
-            prod = dot_lanes(vbuf[j], padded[...])
-            start = pl.multiple_of(slots[j] * blk, blk)
-            remain[:, pl.ds(j * blk, blk)] = ict_ref[:, pl.ds(start, blk)] - prod.T[count:, :]
+        for first in [chunk * c for c, p in enumerate(places) if p == at]:
+            starts = [pl.multiple_of(slots[first + j] * blk, blk) for j in range(chunk)]
+            part = jnp.concatenate([vec_ref[pl.ds(start, blk), :] for start in starts])
+            prod = dot_lanes(picked, part)
+            for j, start in enumerate(starts):
+                remain[:, pl.ds((first + j) * blk, blk)] = (
+                    ict_ref[:, pl.ds(start, blk)] - prod[:, j * blk : (j + 1) * blk]
+                )
         lower[pl.ds(8 * at, 8), :] = eliminate(blocks, at)
     upd_ref[...] = diag_ref[...]
     high, low = halves(remain[...])
@@ -222,19 +220,17 @@
             jax.ShapeDtypeStruct((total, blk), F32),
             jax.ShapeDtypeStruct((copies, blk), F32),
         ),
-        in_specs=[VMEM, VMEM, ANY, VMEM, VMEM, SMEM, SMEM],
+        in_specs=[VMEM, VMEM, VMEM, VMEM, VMEM, SMEM, SMEM],
         out_specs=(VMEM, VMEM, VMEM),
         scratch_shapes=[
-            pltpu.VMEM((most, blk, k), BF16),
             pltpu.VMEM((2 * count, k), BF16),
             pltpu.VMEM((count, LANES), F32),
             pltpu.VMEM((count, most * blk), F32),
             pltpu.SMEM((total + 1,), jnp.int32),
-            pltpu.SemaphoreType.DMA((most,)),
         ],
         compiler_params=pltpu.CompilerParams(vmem_limit_bytes=24 << 20),
         name="step",
-    )(here, there, in_hbm(vec), ict, diag, live, meta)
+    )(here, there, vec, ict, diag, live, meta)
 
 
 def scale_kernel(tops_ref, upd_ref, rel_ref, peak_ref):

time: 75.9 us -> 70.8 us (0.933)
  Pallas kernels: 13.2 us -> 8.2 us
    pallas_call x1, Pallas kernels: 9.9 us -> 4.68 us  [step(): pl.pallas_call(step_kernel, out_shape=(jax.ShapeDtypeStruct((count, rows)...]
where the time goes in v3:
time: 70.8 us; the launch traced here: 70.6 us
  blocking collectives  56.8 us (80%)
  Pallas kernels  8.2 us (12%)
  starting transfers between devices  3.23 us (5%)
  waiting for transfers between devices  1.58 us (2%)
    all_to_all x3, blocking collectives, exchange(): return lax.all_to_all(blocks, axes, split_axis=0, concat_axis=0, tiled=True)  56.8 us
    pallas_call x1, Pallas kernels, step(): pl.pallas_call(step_kernel, out_shape=(jax.ShapeDtypeStruct((count, rows)...  4.68 us
    ppermute x1, starting transfers between devices, on_device(): other = lax.ppermute(placed, 'c', [(0, 1), (1, 0)])  3.23 us
    pallas_call x1, Pallas kernels, pick(): pl.pallas_call(lambda *refs: pick_kernel(count, *refs), out_shape=(jax.Sh...  2.47 us
    ppermute x1, waiting for transfers between devices, on_device(): other = lax.ppermute(placed, 'c', [(0, 1), (1, 0)])  1.58 us
  transfers between devices with their start and end apart: 1, of which 1 were waited for; matrix products, arithmetic and copies ran while one was open for 0% of the time, Pallas kernels for 0%

profile of v3, /device:TPU:1, one launch (start us, length us, event | category | flops | bytes accessed | tf_op | source)
XLA Modules:
  0.0 70.6 jit_solution(5408541635108769362)
XLA Ops:
  0.6 0.0 copy-start
  0.6 2.5 %pick.1 = (f32[8,1,2176]{2,1,0:T(1,128)S(1)}, s32[1]{0:T(128)}) custom-call(s32[1,64]{1,0:T(1,128)} %bitcast.21, s32[16]{0:T(128)} %refs_1_.1, bf16[2048,2048]{1,0:T(8,128)(2,1)} %vec_ref.1, f32[64,2048]{1,0:T(8,128)} %bitcast.15), custom_call_target="tpu_custom_call" | custom-call | tf_op jit(solution)/shard_map/pick/pallas_call | solution.py:83
  3.1 16.2 %all_to_all.21 = f32[8,1,2176]{2,1,0:T(1,128)S(1)} all-to-all(f32[8,1,2176]{2,1,0:T(1,128)S(1)} %get-tuple-element.10), channel_id=1, replica_groups=mesh['z'=8,'y'=4,'c'=2,'x'=4] {'z'}, dimensions={0} | all-to-all | bytes 139264 | tf_op jit(solution)/shard_map/all_to_all | solution.py:257
  19.3 0.1 broadcast_in_dim.7
  19.4 22.6 %all_to_all.22 = f32[16,8,2176]{2,1,0:T(8,128)S(1)} all-to-all(f32[16,8,2176]{2,1,0:T(8,128)S(1)} %broadcast_in_dim.7), channel_id=1, replica_groups=mesh['z'=8,'y'=4,'c'=2,'x'=4] {'y','x'}, dimensions={0} | all-to-all | bytes 2228224 | tf_op jit(solution)/shard_map/all_to_all | solution.py:257
  42.0 0.0 copy-start.1
  42.0 0.0 copy-start.2
  42.0 0.0 copy-start.3
  42.0 0.4 place.1.here_ref
  42.4 3.2 %collective-permute-start = (f32[64,2176]{1,0:T(8,128)S(1)}, f32[64,2176]{1,0:T(8,128)S(1)}, u32[]{:S(2)}, u32[]{:S(2)}) collective-permute-start(f32[64,2176]{1,0:T(8,128)S(1)} %place.1.here_ref), channel_id=1, source_target_pairs={{0,4},{4,0},{1,5},{5,1},{2,6},{6,2},{3,7},{7,3},{8,12},{12,8},{9,1... | collective-permute-start | bytes 1671176 | tf_op jit(solution)/shard_map/ppermute | solution.py:270
  45.6 1.6 %collective-permute-done.there_ref = f32[64,2176]{1,0:T(8,128)S(1)} collective-permute-done((f32[64,2176]{1,0:T(8,128)S(1)}, f32[64,2176]{1,0:T(8,128)S(1)}, u32[]{:S(2)}, u32[]{:S(2)}) %collective-permute-start) | collective-permute-done | bytes 557088 | tf_op jit(solution)/shard_map/ppermute | solution.py:270
  47.2 0.0 copy-done
  47.2 0.0 copy-done.1
  47.2 0.0 copy-done.2
  47.2 0.0 copy-done.3
  47.2 4.7 %step.1 = (f32[64,2048]{1,0:T(8,128)}, f32[16,128]{1,0:T(8,128)S(1)}, f32[256,128]{1,0:T(8,128)S(1)}) custom-call(f32[64,2176]{1,0:T(8,128)S(1)} %place.1.here_ref, f32[64,2176]{1,0:T(8,128)S(1)} %collective-permute-done.there_ref, bf16[2048,2048]{1,0:T(8,128)(2,1)S(1)} %copy-done, f32[64,2048]{1,0:T(8,128)S(1)} %bitcast.16, f32[16,128]{1,0:T(8,128)S(1)} %bitcast.19, ...), custom_call_target="tpu_custom_call" | custom-call | tf_op jit(solution)/shard_map/step/pallas_call | solution.py:216
  51.9 18.0 %all_to_all.23 = f32[256,1,128]{2,1,0:T(1,128)S(1)} all-to-all(f32[256,1,128]{2,1,0:T(1,128)S(1)} %bitcast.18), channel_id=1, replica_groups=mesh['z'=8,'y'=4,'c'=2,'x'=4] {'z','y','c','x'}, dimensions={0} | all-to-all | bytes 262144 | tf_op jit(solution)/shard_map/all_to_all | solution.py:257
  69.9 0.7 scale.1
  (1 shorter events, 0.0 us)
Async XLA Ops:
  0.6 46.6 %copy-start = (bf16[2048,2048]{1,0:T(8,128)(2,1)S(1)}, bf16[2048,2048]{1,0:T(8,128)(2,1)}, u32[]{:S(2)}) copy-start(bf16[2048,2048]{1,0:T(8,128)(2,1)} %vec_ref.1) | copy-start | bytes 25165828
  42.0 5.2 %copy-start.1 = (f32[2048,64]{0,1:T(8,128)S(1)}, f32[2048,64]{0,1:T(8,128)}, u32[]{:S(2)}) copy-start(f32[2048,64]{0,1:T(8,128)} %param.7) | copy-start | bytes 1572868
  42.0 5.2 %copy-start.2 = (f32[2048]{0:T(1024)S(1)}, f32[2048]{0:T(1024)}, u32[]{:S(2)}) copy-start(f32[2048]{0:T(1024)} %param.8) | copy-start | bytes 24580
  42.0 5.2 %copy-start.3 = (s32[16]{0:T(128)S(1)}, s32[16]{0:T(128)}, u32[]{:S(2)}) copy-start(s32[16]{0:T(128)} %live_ref.1) | copy-start | bytes 196
  42.4 4.8 %collective-permute-start = (f32[64,2176]{1,0:T(8,128)S(1)}, f32[64,2176]{1,0:T(8,128)S(1)}, u32[]{:S(2)}, u32[]{:S(2)}) collective-permute-start(f32[64,2176]{1,0:T(8,128)S(1)} %place.1.here_ref), channel_id=1, source_target_pairs={{0,4},{4,0},{1,5},{5,1},{2,6},{6,2},{3,7},{7,3},{8,12},{12,8},{9,1... | collective-permute-start | bytes 1671176 | tf_op jit(solution)/shard_map/ppermute | solution.py:270

commit v4 on v3

--- a/solution.py
+++ b/solution.py
@@ -1,5 +1,9 @@
+import functools
+import math
+
 import jax
 import jax.numpy as jnp
+import numpy as np
 from jax import lax
 from jax.experimental import pallas as pl
 from jax.experimental.pallas import tpu as pltpu
@@ -37,7 +41,9 @@
     return hi, (a - hi.astype(F32)).astype(BF16)
 
 
-def pick_kernel(count, piv_ref, spb_ref, vec_ref, ict_ref, out_ref, meta_ref, vbuf, ibuf, sems):
+def pick_kernel(
+    count, piv_ref, spb_ref, live_ref, vec_ref, ict_ref, out_ref, plan_ref, vbuf, ibuf, sems
+):
     piv = piv_ref[...]
     group, offset = piv >> 7, piv & (LANES - 1)
     code = jnp.zeros(piv.shape, jnp.int32)
@@ -59,7 +65,14 @@
     )
     vcopy.start()
     icopy.start()
-    meta_ref[0] = jnp.where(has, row, -1)
+    total = live_ref.shape[0]
+    found = jnp.int32(0)
+    for wanted in (1, 0):
+        for s in range(total):
+            plan_ref[found] = s
+            plan_ref[total + found] = wanted
+            found += (live_ref[s] > 0) == (wanted > 0)
+    plan_ref[2 * total] = jnp.where(has, row, -1)
     ibuf[pl.ds(0, count), :] = jnp.zeros((count, LANES), F32)
     k = vbuf.shape[1]
     vcopy.wait()
@@ -78,15 +91,15 @@
         out_ref[i, :, pl.ds(k, LANES)] = tail
 
 
-def pick(pivots, spb, vec, ict, copies):
+def pick(pivots, spb, live, vec, ict, copies):
     count, k = pivots.shape[1], vec.shape[1]
     return pl.pallas_call(
         lambda *refs: pick_kernel(count, *refs),
         out_shape=(
             jax.ShapeDtypeStruct((copies, 1, k + LANES), F32),
-            jax.ShapeDtypeStruct((1,), jnp.int32),
+            pltpu.SMEM((2 * live.shape[0] + 2,), jnp.int32),
         ),
-        in_specs=[VMEM, SMEM, ANY, ANY],
+        in_specs=[VMEM, SMEM, SMEM, ANY, ANY],
         out_specs=(VMEM, SMEM),
         scratch_shapes=[
             pltpu.VMEM((8, k), BF16),
@@ -95,7 +108,7 @@
         ],
         compiler_params=pltpu.CompilerParams(vmem_limit_bytes=8 << 20),
         name="pick",
-    )(in_hbm(pivots), in_hbm(spb), in_hbm(vec), in_hbm(ict))
+    )(in_hbm(pivots), in_hbm(spb), in_hbm(live), in_hbm(vec), in_hbm(ict))
 
 
 def place_kernel(rows_ref, out_ref):
@@ -152,21 +165,14 @@
 
 
 def step_kernel(
-    here_ref, there_ref, vec_ref, ict_ref, diag_ref, live_ref, meta_ref,
+    here_ref, there_ref, vec_ref, ict_ref, diag_ref, plan_ref,
     cols_ref, upd_ref, top_ref,
-    padded, lower, remain, slots,
+    padded, lower, remain,
 ):
-    count, total = here_ref.shape[0], live_ref.shape[0]
+    count, total = here_ref.shape[0], diag_ref.shape[0]
     k = vec_ref.shape[1]
     blk = vec_ref.shape[0] // total
     most = remain.shape[1] // blk
-    found = jnp.int32(0)
-    for s in range(total):
-        slots[found] = s
-        found += live_ref[s]
-    for s in range(total):
-        slots[found] = s
-        found += 1 - live_ref[s]
     cols_ref[...] = jnp.zeros(cols_ref.shape, F32)
     picked = (here_ref[:, pl.ds(0, k)] + there_ref[:, pl.ds(0, k)]).astype(BF16)
     padded[pl.ds(0, count), :] = jnp.zeros((count, k), BF16)
@@ -179,10 +185,10 @@
     panels = count // 8
     blocks = [whole[8 * i : 8 * i + 8] for i in range(panels)]
     chunk = 4
-    places = [1, 3, 5]
+    places = [0, 1, 2]
     for at in range(panels):
         for first in [chunk * c for c, p in enumerate(places) if p == at]:
-            starts = [pl.multiple_of(slots[first + j] * blk, blk) for j in range(chunk)]
+            starts = [pl.multiple_of(plan_ref[first + j] * blk, blk) for j in range(chunk)]
             part = jnp.concatenate([vec_ref[pl.ds(start, blk), :] for start in starts])
             prod = dot_lanes(picked, part)
             for j, start in enumerate(starts):
@@ -196,89 +202,102 @@
     cols = dot(lhigh, high) + dot(lhigh, low) + dot(llow, high)
     top = jnp.zeros((1, blk), F32)
     for j in range(most):
-        s = slots[j]
-        live = live_ref[s] > 0
+        s = plan_ref[j]
+        live = plan_ref[total + j] > 0
         mine = cols[:, j * blk : (j + 1) * blk]
         left = diag_ref[pl.ds(s, 1), :] - jnp.sum(mine * mine, axis=0, keepdims=True)
-        left = jnp.where(iota((1, blk), 1) + s * blk == meta_ref[0], 0.0, left)
+        left = jnp.where(iota((1, blk), 1) + s * blk == plan_ref[2 * total], 0.0, left)
         cols_ref[:, pl.ds(pl.multiple_of(s * blk, blk), blk)] = jnp.where(live, mine, 0.0)
         upd_ref[pl.ds(s, 1), :] = jnp.where(live, left, diag_ref[pl.ds(s, 1), :])
         top = jnp.maximum(top, jnp.where(live, left, 0.0))
     top_ref[...] = jnp.broadcast_to(top, top_ref.shape)
 
 
-def step(here, there, vec, ict, diag, live, meta, copies):
+def step(here, there, vec, ict, diag, plan, copies):
     count, rows = ict.shape
     k = vec.shape[1]
-    total = live.shape[0]
+    total = diag.shape[0]
     blk = rows // total
     most = min(LIVE_MOST, total)
     return pl.pallas_call(
         step_kernel,
         out_shape=(
-            jax.ShapeDtypeStruct((count, rows), F32),
-            jax.ShapeDtypeStruct((total, blk), F32),
-            jax.ShapeDtypeStruct((copies, blk), F32),
+            pltpu.VMEM((count, rows), F32),
+            pltpu.VMEM((total, blk), F32),
+            pltpu.VMEM((copies, blk), F32),
         ),
-        in_specs=[VMEM, VMEM, VMEM, VMEM, VMEM, SMEM, SMEM],
+        in_specs=[VMEM, VMEM, VMEM, VMEM, VMEM, SMEM],
         out_specs=(VMEM, VMEM, VMEM),
         scratch_shapes=[
             pltpu.VMEM((2 * count, k), BF16),
             pltpu.VMEM((count, LANES), F32),
             pltpu.VMEM((count, most * blk), F32),
-            pltpu.SMEM((total + 1,), jnp.int32),
         ],
         compiler_params=pltpu.CompilerParams(vmem_limit_bytes=24 << 20),
         name="step",
-    )(here, there, vec, ict, diag, live, meta)
-
-
-def scale_kernel(tops_ref, upd_ref, rel_ref, peak_ref):
+    )(here, there, vec, ict, diag, plan)
+
+
+def scale_kernel(tops_ref, upd_ref, held_ref, cols_ref, rel_ref, peak_ref, sem):
+    leaving = pltpu.make_async_copy(held_ref, cols_ref, sem)
+    leaving.start()
     peak = jnp.max(jnp.max(tops_ref[...], axis=0, keepdims=True), axis=1, keepdims=True)
     rel_ref[...] = upd_ref[...] / peak
     peak_ref[...] = peak
-
-
-def scale(tops, upd):
+    leaving.wait()
+
+
+def scale(tops, upd, cols):
     return pl.pallas_call(
         scale_kernel,
         out_shape=(
+            jax.ShapeDtypeStruct(cols.shape, F32),
             jax.ShapeDtypeStruct(upd.shape, F32),
             jax.ShapeDtypeStruct((1, 1), F32),
         ),
-        in_specs=[VMEM, VMEM],
-        out_specs=(VMEM, VMEM),
+        in_specs=[VMEM, VMEM, VMEM],
+        out_specs=(ANY, VMEM, VMEM),
+        scratch_shapes=[pltpu.SemaphoreType.DMA],
         compiler_params=pltpu.CompilerParams(vmem_limit_bytes=4 << 20),
         name="scale",
-    )(tops, upd)
-
-
-def exchange(blocks, axes):
-    return lax.all_to_all(blocks, axes, split_axis=0, concat_axis=0, tiled=True)
-
-
-def on_device(vec, ints, diag, spb, live, pivots):
+    )(tops, upd, cols)
+
+
+def exchange(blocks, groups=None):
+    return lax.all_to_all(
+        blocks, "d", split_axis=0, concat_axis=0, axis_index_groups=groups, tiled=True
+    )
+
+
+def on_device(shape, vec, ints, diag, spb, live, pivots):
     count = pivots.shape[0]
     ict = ints.T
-    sizes = {a: lax.axis_size(a) for a in AXES}
-    near = sizes["y"] * sizes["x"]
-    mine, meta = pick(pivots[None, :], spb, vec, ict, sizes["z"])
-    column = exchange(mine, "z")
-    column = column.reshape(column.shape[0], -1)
-    rows = exchange(jnp.broadcast_to(column, (near, *column.shape)), ("y", "x"))
+    at = np.arange(math.prod(shape)).reshape(shape)
+    wide = [at[:, :, 0, x].ravel().tolist() for x in range(shape[3])]
+    wide += [at[:, y, 1, :].ravel().tolist() for y in range(shape[1])]
+    near = [at[z, y, 0, :].tolist() for z in range(shape[0]) for y in range(shape[1])]
+    near += [at[z, :, 1, x].tolist() for z in range(shape[0]) for x in range(shape[3])]
+    mine, plan = pick(pivots[None, :], spb, live, vec, ict, len(wide[0]))
+    sheet = exchange(mine, wide).reshape(len(wide[0]), -1)
+    rows = exchange(jnp.broadcast_to(sheet, (len(near[0]), *sheet.shape)), near)
     placed = place(rows.reshape(-1, rows.shape[-1]), count)
-    other = lax.ppermute(placed, "c", [(0, 1), (1, 0)])
+    pairs = [(int(p), int(q)) for p, q in zip(at.ravel(), at[:, :, ::-1].ravel())]
+    other = lax.ppermute(placed, "d", pairs)
     cols, upd, top = step(
-        placed, other, vec, ict, diag.reshape(live.shape[0], -1), live, meta, near * sizes["z"] * sizes["c"]
-    )
-    rel, peak = scale(exchange(top, AXES), upd)
+        placed, other, vec, ict, diag.reshape(live.shape[0], -1), plan, at.size
+    )
+    cols, rel, peak = scale(exchange(top), upd, cols)
     return (cols.T, rel.reshape(-1), peak.reshape(()))
 
 
 def solution(mesh):
-    split = Mesh(mesh.devices.reshape(8, 4, 2, mesh.shape["grp"]), AXES)
-    in_specs = (P(AXES, None), P(AXES, None), P(AXES), P(AXES), P(AXES), P())
-    out_specs = (P(AXES, None), P(AXES), P())
+    shape = (8, 4, 2, mesh.shape["grp"])
+    flat = Mesh(mesh.devices.reshape(-1), ("d",))
+    d = P("d")
     return jax.shard_map(
-        on_device, mesh=split, in_specs=in_specs, out_specs=out_specs, check_vma=False
-    )
+        functools.partial(on_device, shape),
+        mesh=flat,
+        in_specs=(d, d, d, d, d, P()),
+        out_specs=(d, d, P()),
+        check_vma=False,
+    )

time: 70.8 us -> 69 us (0.975)
  Pallas kernels: 8.2 us -> 6.82 us
  blocking collectives: 56.8 us -> 56 us
    pallas_call x2, Pallas kernels: 5.38 us -> 4.27 us  [the longest x1 2.86 us: step(): pl.pallas_call(step_kernel, out_shape=(pltpu.VMEM((count, rows), F32), pl...]
    all_to_all x3, blocking collectives: 56.8 us -> 56 us  [exchange(): lax.all_to_all(blocks, 'd', split_axis=0, concat_axis=0, axis_index_group...]
where the time goes in v4:
time: 69 us; the launch traced here: 68.8 us
  blocking collectives  56 us (81%)
  Pallas kernels  6.82 us (10%)
  starting transfers between devices  3.64 us (5%)
  waiting for transfers between devices  1.58 us (2%)
    all_to_all x3, blocking collectives, exchange(): lax.all_to_all(blocks, 'd', split_axis=0, concat_axis=0, axis_index_group...  56 us
    ppermute x1, starting transfers between devices, on_device(): other = lax.ppermute(placed, 'd', pairs)  3.64 us
    pallas_call x1, Pallas kernels, step(): pl.pallas_call(step_kernel, out_shape=(pltpu.VMEM((count, rows), F32), pl...  2.86 us
    pallas_call x1, Pallas kernels, pick(): pl.pallas_call(lambda *refs: pick_kernel(count, *refs), out_shape=(jax.Sh...  2.2 us
    ppermute x1, waiting for transfers between devices, on_device(): other = lax.ppermute(placed, 'd', pairs)  1.58 us
    pallas_call x1, Pallas kernels, scale(): pl.pallas_call(scale_kernel, out_shape=(jax.ShapeDtypeStruct(cols.shape,...  1.41 us
  transfers between devices with their start and end apart: 1, of which 1 were waited for; matrix products, arithmetic and copies ran while one was open for 0% of the time, Pallas kernels for 0%

profile of v4, /device:TPU:1, one launch (start us, length us, event | category | flops | bytes accessed | tf_op | source)
XLA Modules:
  0.0 68.8 jit_solution(3481554530952504823)
XLA Ops:
  0.6 0.0 copy-start
  0.6 2.2 %pick.1 = (f32[32,1,2176]{2,1,0:T(1,128)S(1)}, s32[34]{0:T(128)S(4)}) custom-call(s32[1,64]{1,0:T(1,128)} %bitcast.21, s32[16]{0:T(128)} %refs_1_.1, s32[16]{0:T(128)} %refs_2_.1, bf16[2048,2048]{1,0:T(8,128)(2,1)} %vec_ref.1, f32[64,2048]{1,0:T(8,128)} %bitcast.15), custom_call_target="tpu_custom_call" | custom-call | tf_op jit(solution)/shard_map/pick/pallas_call | solution.py:96
  2.8 23.5 %all_to_all.21 = f32[32,1,2176]{2,1,0:T(1,128)S(1)} all-to-all(f32[32,1,2176]{2,1,0:T(1,128)S(1)} %get-tuple-element.11), channel_id=1, replica_groups={{0,8,16,24,32,40,48,56,64,72,80,88,96,104,112,120,128,136,144,152,160,1..., dimensions={0} | all-to-all | bytes 557056 | tf_op jit(solution)/shard_map/all_to_all | solution.py:267
  26.4 0.1 broadcast_in_dim.7
  26.5 14.4 %all_to_all.22 = f32[4,32,2176]{2,1,0:T(8,128)S(1)} all-to-all(f32[4,32,2176]{2,1,0:T(8,128)S(1)} %broadcast_in_dim.7), channel_id=1, replica_groups={{0,1,2,3},{8,9,10,11},{16,17,18,19},{24,25,26,27},{32,33,34,35},{40,41,..., dimensions={0} | all-to-all | bytes 2228224 | tf_op jit(solution)/shard_map/all_to_all | solution.py:267
  40.9 0.0 copy-start.1
  40.9 0.0 copy-start.2
  40.9 0.4 place.1.here_ref
  41.2 3.6 %collective-permute-start = (f32[64,2176]{1,0:T(8,128)S(1)}, f32[64,2176]{1,0:T(8,128)S(1)}, u32[]{:S(2)}, u32[]{:S(2)}) collective-permute-start(f32[64,2176]{1,0:T(8,128)S(1)} %place.1.here_ref), channel_id=1, source_target_pairs={{0,4},{1,5},{2,6},{3,7},{4,0},{5,1},{6,2},{7,3},{8,12},{9,13},{10,... | collective-permute-start | bytes 1671176 | tf_op jit(solution)/shard_map/ppermute | solution.py:285
  44.9 1.6 %collective-permute-done.there_ref = f32[64,2176]{1,0:T(8,128)S(1)} collective-permute-done((f32[64,2176]{1,0:T(8,128)S(1)}, f32[64,2176]{1,0:T(8,128)S(1)}, u32[]{:S(2)}, u32[]{:S(2)}) %collective-permute-start) | collective-permute-done | bytes 557088 | tf_op jit(solution)/shard_map/ppermute | solution.py:285
  46.5 0.0 copy-done
  46.5 0.0 copy-done.1
  46.5 0.0 copy-done.2
  46.5 2.9 %step.1 = (f32[64,2048]{1,0:T(8,128)S(1)}, f32[16,128]{1,0:T(8,128)S(1)}, f32[256,128]{1,0:T(8,128)S(1)}) custom-call(f32[64,2176]{1,0:T(8,128)S(1)} %place.1.here_ref, f32[64,2176]{1,0:T(8,128)S(1)} %collective-permute-done.there_ref, bf16[2048,2048]{1,0:T(8,128)(2,1)S(1)} %copy-done, f32[64,2048]{1,0:T(8,128)S(1)} %bitcast.16, f32[16,128]{1,0:T(8,128)S(1)} %bitcast.19, ...), custom_call_target="tpu_custom_call" | custom-call | tf_op jit(solution)/shard_map/step/pallas_call | solution.py:222
  49.4 18.0 %all_to_all.23 = f32[256,1,128]{2,1,0:T(1,128)S(1)} all-to-all(f32[256,1,128]{2,1,0:T(1,128)S(1)} %bitcast.18), channel_id=1, replica_groups=mesh['rows'=64,'grp'=4] {'rows','grp'}, dimensions={0} | all-to-all | bytes 262144 | tf_op jit(solution)/shard_map/all_to_all | solution.py:267
  67.4 1.4 %scale.1 = (f32[64,2048]{1,0:T(8,128)}, f32[16,128]{1,0:T(8,128)}, f32[1,1]{1,0:T(1,128)}) custom-call(f32[256,128]{1,0:T(8,128)S(1)} %bitcast.17, f32[16,128]{1,0:T(8,128)S(1)} %get-tuple-element.14.upd_ref, f32[64,2048]{1,0:T(8,128)S(1)} %get-tuple-element.15.held_ref), custom_call_target="tpu_custom_call" | custom-call | tf_op jit(solution)/shard_map/scale/pallas_call | solution.py:251
  (1 shorter events, 0.0 us)
Async XLA Ops:
  0.6 45.8 %copy-start = (bf16[2048,2048]{1,0:T(8,128)(2,1)S(1)}, bf16[2048,2048]{1,0:T(8,128)(2,1)}, u32[]{:S(2)}) copy-start(bf16[2048,2048]{1,0:T(8,128)(2,1)} %vec_ref.1) | copy-start | bytes 25165828
  40.9 5.6 %copy-start.1 = (f32[2048,64]{0,1:T(8,128)S(1)}, f32[2048,64]{0,1:T(8,128)}, u32[]{:S(2)}) copy-start(f32[2048,64]{0,1:T(8,128)} %param.7) | copy-start | bytes 1572868
  40.9 5.6 %copy-start.2 = (f32[2048]{0:T(1024)S(1)}, f32[2048]{0:T(1024)}, u32[]{:S(2)}) copy-start(f32[2048]{0:T(1024)} %param.8) | copy-start | bytes 24580
  41.2 5.2 %collective-permute-start = (f32[64,2176]{1,0:T(8,128)S(1)}, f32[64,2176]{1,0:T(8,128)S(1)}, u32[]{:S(2)}, u32[]{:S(2)}) collective-permute-start(f32[64,2176]{1,0:T(8,128)S(1)} %place.1.here_ref), channel_id=1, source_target_pairs={{0,4},{1,5},{2,6},{3,7},{4,0},{5,1},{6,2},{7,3},{8,12},{9,13},{10,... | collective-permute-start | bytes 1671176 | tf_op jit(solution)/shard_map/ppermute | solution.py:285

commit v5 on v4

--- a/solution.py
+++ b/solution.py
@@ -28,8 +28,8 @@
     return pltpu.with_memory_space_constraint(a, pltpu.HBM)
 
 
-def dot_lanes(a, b, **kw):
-    return lax.dot_general(a, b, (((1,), (1,)), ((), ())), preferred_element_type=F32, **kw)
+def dot_lanes(a, b):
+    return lax.dot_general(a, b, (((1,), (1,)), ((), ())), preferred_element_type=F32)
 
 
 def dot(a, b):
@@ -83,8 +83,12 @@
         out_ref[i, :, pl.ds(0, k)] = vrow
     icopy.wait()
     tile = (8, LANES)
-    hot = jnp.where((iota(tile, 1) == row % LANES) & has, 1.0, 0.0)
-    ints = dot_lanes(hot, ibuf[...], precision=lax.Precision.HIGHEST)
+    hot = jnp.where((iota(tile, 1) == row % LANES) & has, 1.0, 0.0).astype(BF16)
+    rest, ints = ibuf[...], jnp.zeros(tile, F32)
+    for _ in range(3):
+        part = rest.astype(BF16)
+        rest = rest - part.astype(F32)
+        ints += dot_lanes(hot, part)
     index = jnp.where(has, q + 1, 0).astype(F32)
     tail = jnp.where(iota(tile, 1) == 0, index, ints)[0:1]
     for i in range(copies):
@@ -111,16 +115,21 @@
     )(in_hbm(pivots), in_hbm(spb), in_hbm(live), in_hbm(vec), in_hbm(ict))
 
 
-def place_kernel(rows_ref, out_ref):
-    k = rows_ref.shape[1] - LANES
-    tail = rows_ref[:, pl.ds(k, LANES)]
-    hot = tail[:, 0:1].astype(jnp.int32) - 1 == iota((rows_ref.shape[0], out_ref.shape[0]), 1)
-    hot = jnp.where(hot, 1.0, 0.0).astype(BF16)
+def place_kernel(*refs):
+    *sheets, out_ref = refs
+    k = out_ref.shape[1] - LANES
     turn = (((0,), (0,)), ((), ()))
-    out_ref[:, pl.ds(0, k)] = lax.dot_general(
-        hot, rows_ref[:, pl.ds(0, k)].astype(BF16), turn, preferred_element_type=F32
-    )
     total = jnp.zeros((out_ref.shape[0], LANES), F32)
+    hots = []
+    tails = []
+    for ref in sheets:
+        tail = ref[:, pl.ds(k, LANES)]
+        hot = tail[:, 0:1].astype(jnp.int32) - 1 == iota((ref.shape[0], out_ref.shape[0]), 1)
+        hots.append(jnp.where(hot, 1.0, 0.0).astype(BF16))
+        tails.append(tail)
+    hot, tail = jnp.concatenate(hots), jnp.concatenate(tails)
+    body = jnp.concatenate([ref[:, pl.ds(0, k)].astype(BF16) for ref in sheets])
+    out_ref[:, pl.ds(0, k)] = lax.dot_general(hot, body, turn, preferred_element_type=F32)
     for _ in range(3):
         part = tail.astype(BF16)
         tail = tail - part.astype(F32)
@@ -128,15 +137,15 @@
     out_ref[:, pl.ds(k, LANES)] = total
 
 
-def place(rows, count):
+def place(sheets, count):
     return pl.pallas_call(
         place_kernel,
-        out_shape=jax.ShapeDtypeStruct((count, rows.shape[1]), F32),
-        in_specs=[VMEM],
+        out_shape=jax.ShapeDtypeStruct((count, sheets[0].shape[1]), F32),
+        in_specs=[VMEM] * len(sheets),
         out_specs=VMEM,
         compiler_params=pltpu.CompilerParams(vmem_limit_bytes=8 << 20),
         name="place",
-    )(rows)
+    )(*sheets)
 
 
 def eliminate(blocks, at):
@@ -238,13 +247,23 @@
     )(here, there, vec, ict, diag, plan)
 
 
-def scale_kernel(tops_ref, upd_ref, held_ref, cols_ref, rel_ref, peak_ref, sem):
-    leaving = pltpu.make_async_copy(held_ref, cols_ref, sem)
-    leaving.start()
+def scale_kernel(tops_ref, upd_ref, held_ref, cols_ref, rel_ref, peak_ref, rel, top, sems):
+    leaving = []
+    for i, part in enumerate((pl.ds(0, 8), pl.ds(8, held_ref.shape[0] - 8))):
+        leaving.append(
+            pltpu.make_async_copy(held_ref.at[part, :], cols_ref.at[part, :], sems.at[i])
+        )
+        leaving[-1].start()
     peak = jnp.max(jnp.max(tops_ref[...], axis=0, keepdims=True), axis=1, keepdims=True)
-    rel_ref[...] = upd_ref[...] / peak
-    peak_ref[...] = peak
-    leaving.wait()
+    rel[...] = upd_ref[...] / peak
+    top[...] = peak
+    leaving.pop(0).wait()
+    leaving.append(pltpu.make_async_copy(rel, rel_ref, sems.at[2]))
+    leaving.append(pltpu.make_async_copy(top, peak_ref, sems.at[3]))
+    leaving[-2].start()
+    leaving[-1].start()
+    for copy in leaving:
+        copy.wait()
 
 
 def scale(tops, upd, cols):
@@ -256,8 +275,12 @@
             jax.ShapeDtypeStruct((1, 1), F32),
         ),
         in_specs=[VMEM, VMEM, VMEM],
-        out_specs=(ANY, VMEM, VMEM),
-        scratch_shapes=[pltpu.SemaphoreType.DMA],
+        out_specs=(ANY, ANY, ANY),
+        scratch_shapes=[
+            pltpu.VMEM(upd.shape, F32),
+            pltpu.VMEM((1, 1), F32),
+            pltpu.SemaphoreType.DMA((4,)),
+        ],
         compiler_params=pltpu.CompilerParams(vmem_limit_bytes=4 << 20),
         name="scale",
     )(tops, upd, cols)
@@ -275,12 +298,14 @@
     at = np.arange(math.prod(shape)).reshape(shape)
     wide = [at[:, :, 0, x].ravel().tolist() for x in range(shape[3])]
     wide += [at[:, y, 1, :].ravel().tolist() for y in range(shape[1])]
-    near = [at[z, y, 0, :].tolist() for z in range(shape[0]) for y in range(shape[1])]
-    near += [at[z, :, 1, x].tolist() for z in range(shape[0]) for x in range(shape[3])]
+    turns = []
+    for k in range(1, shape[3]):
+        to = np.stack([np.roll(at[:, :, 0], -k, 2), np.roll(at[:, :, 1], -k, 1)], 2)
+        turns.append([(int(p), int(q)) for p, q in zip(at.ravel(), to.ravel())])
     mine, plan = pick(pivots[None, :], spb, live, vec, ict, len(wide[0]))
     sheet = exchange(mine, wide).reshape(len(wide[0]), -1)
-    rows = exchange(jnp.broadcast_to(sheet, (len(near[0]), *sheet.shape)), near)
-    placed = place(rows.reshape(-1, rows.shape[-1]), count)
+    sheets = [sheet] + [lax.ppermute(sheet, "d", turn) for turn in turns]
+    placed = place(sheets, count)
     pairs = [(int(p), int(q)) for p, q in zip(at.ravel(), at[:, :, ::-1].ravel())]
     other = lax.ppermute(placed, "d", pairs)
     cols, upd, top = step(

time: 69 us -> 67.3 us (0.975)
  blocking collectives: 56 us -> 41.5 us
  waiting for transfers between devices: 1.58 us -> 10.8 us
  starting transfers between devices: 3.64 us -> 7.24 us
    all_to_all x3 -> x2, blocking collectives: 56 us -> 41.5 us  [exchange(): lax.all_to_all(blocks, 'd', split_axis=0, concat_axis=0, axis_index_group...]
    ppermute x0 -> x3, waiting for transfers between devices: none -> 9.21 us  [on_device(): sheets = [sheet] + [lax.ppermute(sheet, 'd', turn) for turn in turns]]
    ppermute x0 -> x3, starting transfers between devices: none -> 3.85 us  [on_device(): sheets = [sheet] + [lax.ppermute(sheet, 'd', turn) for turn in turns]]
  transfers between devices with their start and end apart: 1 -> 4, of which waited for: 1 -> 4; matrix products, arithmetic and copies ran while one was open for 0% -> 0% of each run, Pallas kernels for 0% -> 0%
where the time goes in v5:
time: 67.3 us; the launch traced here: 67.2 us
  blocking collectives  41.5 us (62%)
  waiting for transfers between devices  10.8 us (16%)
  starting transfers between devices  7.24 us (11%)
  Pallas kernels  6.88 us (10%)
  between operations  0.69 us (1%)
    all_to_all x2, blocking collectives, exchange(): lax.all_to_all(blocks, 'd', split_axis=0, concat_axis=0, axis_index_group...  41.5 us
    ppermute x3, waiting for transfers between devices, on_device(): sheets = [sheet] + [lax.ppermute(sheet, 'd', turn) for turn in turns]  9.21 us
    ppermute x3, starting transfers between devices, on_device(): sheets = [sheet] + [lax.ppermute(sheet, 'd', turn) for turn in turns]  3.85 us
    ppermute x1, starting transfers between devices, on_device(): other = lax.ppermute(placed, 'd', pairs)  3.4 us
    pallas_call x1, Pallas kernels, step(): pl.pallas_call(step_kernel, out_shape=(pltpu.VMEM((count, rows), F32), pl...  2.87 us
    pallas_call x1, Pallas kernels, pick(): pl.pallas_call(lambda *refs: pick_kernel(count, *refs), out_shape=(jax.Sh...  2.4 us
    ppermute x1, waiting for transfers between devices, on_device(): other = lax.ppermute(placed, 'd', pairs)  1.58 us
  transfers between devices with their start and end apart: 4, of which 4 were waited for; matrix products, arithmetic and copies ran while one was open for 0% of the time, Pallas kernels for 0%

profile of v5, /device:TPU:1, one launch (start us, length us, event | category | flops | bytes accessed | tf_op | source)
XLA Modules:
  0.0 67.2 jit_solution(7255778581186793592)
XLA Ops:
  0.6 0.0 copy-start
  0.6 0.0 copy-start.1
  0.7 0.0 copy-start.2
  0.7 2.4 %pick.1 = (f32[32,1,2176]{2,1,0:T(1,128)S(1)}, s32[34]{0:T(128)S(4)}) custom-call(s32[1,64]{1,0:T(1,128)} %bitcast.22, s32[16]{0:T(128)} %refs_1_.1, s32[16]{0:T(128)} %refs_2_.1, bf16[2048,2048]{1,0:T(8,128)(2,1)} %vec_ref.1, f32[64,2048]{1,0:T(8,128)} %bitcast.13), custom_call_target="tpu_custom_call" | custom-call | tf_op jit(solution)/shard_map/pick/pallas_call | solution.py:100
  3.1 23.5 %all_to_all.16 = f32[32,1,2176]{2,1,0:T(1,128)S(1)} all-to-all(f32[32,1,2176]{2,1,0:T(1,128)S(1)} %get-tuple-element.11), channel_id=1, replica_groups={{0,8,16,24,32,40,48,56,64,72,80,88,96,104,112,120,128,136,144,152,160,1..., dimensions={0} | all-to-all | bytes 557056 | tf_op jit(solution)/shard_map/all_to_all | solution.py:290
  26.6 3.2 %collective-permute-start.2 = (f32[32,2176]{1,0:T(8,128)S(1)}, f32[32,2176]{1,0:T(8,128)S(1)}, u32[]{:S(2)}, u32[]{:S(2)}) collective-permute-start(f32[32,2176]{1,0:T(8,128)S(1)} %bitcast.15), channel_id=1, source_target_pairs={{0,3},{1,0},{2,1},{3,2},{4,28},{5,29},{6,30},{7,31},{8,11},{9,8},{... | collective-permute-start | bytes 835592 | tf_op jit(solution)/shard_map/ppermute | solution.py:307
  29.8 0.0 collective-permute-start.1
  29.8 0.7 %collective-permute-start = (f32[32,2176]{1,0:T(8,128)S(1)}, f32[32,2176]{1,0:T(8,128)S(1)}, u32[]{:S(2)}, u32[]{:S(2)}) collective-permute-start(f32[32,2176]{1,0:T(8,128)S(1)} %bitcast.17), channel_id=1, source_target_pairs={{0,1},{1,2},{2,3},{3,0},{4,12},{5,13},{6,14},{7,15},{8,9},{9,10},{... | collective-permute-start | bytes 835592 | tf_op jit(solution)/shard_map/ppermute | solution.py:307
  30.5 5.8 %collective-permute-done.2.refs_3_ = f32[32,2176]{1,0:T(8,128)S(1)} collective-permute-done((f32[32,2176]{1,0:T(8,128)S(1)}, f32[32,2176]{1,0:T(8,128)S(1)}, u32[]{:S(2)}, u32[]{:S(2)}) %collective-permute-start.2) | collective-permute-done | bytes 278560 | tf_op jit(solution)/shard_map/ppermute | solution.py:307
  36.3 0.8 %collective-permute-done.1.refs_2_ = f32[32,2176]{1,0:T(8,128)S(1)} collective-permute-done((f32[32,2176]{1,0:T(8,128)S(1)}, f32[32,2176]{1,0:T(8,128)S(1)}, u32[]{:S(2)}, u32[]{:S(2)}) %collective-permute-start.1) | collective-permute-done | bytes 278560 | tf_op jit(solution)/shard_map/ppermute | solution.py:307
  37.0 2.6 %collective-permute-done.refs_1_ = f32[32,2176]{1,0:T(8,128)S(1)} collective-permute-done((f32[32,2176]{1,0:T(8,128)S(1)}, f32[32,2176]{1,0:T(8,128)S(1)}, u32[]{:S(2)}, u32[]{:S(2)}) %collective-permute-start) | collective-permute-done | bytes 278560 | tf_op jit(solution)/shard_map/ppermute | solution.py:307
  39.7 0.4 place.1.here_ref
  40.0 3.4 %collective-permute-start.3 = (f32[64,2176]{1,0:T(8,128)S(1)}, f32[64,2176]{1,0:T(8,128)S(1)}, u32[]{:S(2)}, u32[]{:S(2)}) collective-permute-start(f32[64,2176]{1,0:T(8,128)S(1)} %place.1.here_ref), channel_id=1, source_target_pairs={{0,4},{1,5},{2,6},{3,7},{4,0},{5,1},{6,2},{7,3},{8,12},{9,13},{10,... | collective-permute-start | bytes 1671176 | tf_op jit(solution)/shard_map/ppermute | solution.py:310
  43.4 1.6 %collective-permute-done.3.there_ref = f32[64,2176]{1,0:T(8,128)S(1)} collective-permute-done((f32[64,2176]{1,0:T(8,128)S(1)}, f32[64,2176]{1,0:T(8,128)S(1)}, u32[]{:S(2)}, u32[]{:S(2)}) %collective-permute-start.3) | collective-permute-done | bytes 557088 | tf_op jit(solution)/shard_map/ppermute | solution.py:310
  45.0 0.0 copy-done
  45.0 0.0 copy-done.1
  45.0 0.0 copy-done.2
  45.0 2.9 %step.1 = (f32[64,2048]{1,0:T(8,128)S(1)}, f32[16,128]{1,0:T(8,128)S(1)}, f32[256,128]{1,0:T(8,128)S(1)}) custom-call(f32[64,2176]{1,0:T(8,128)S(1)} %place.1.here_ref, f32[64,2176]{1,0:T(8,128)S(1)} %collective-permute-done.3.there_ref, bf16[2048,2048]{1,0:T(8,128)(2,1)S(1)} %copy-done, f32[64,2048]{1,0:T(8,128)S(1)} %bitcast.14, f32[16,128]{1,0:T(8,128)S(1)} %bitcast.21, ...), custom_call_target="tpu_custom_call" | custom-call | tf_op jit(solution)/shard_map/step/pallas_call | solution.py:231
  47.9 18.0 %all_to_all.17 = f32[256,1,128]{2,1,0:T(1,128)S(1)} all-to-all(f32[256,1,128]{2,1,0:T(1,128)S(1)} %bitcast.20), channel_id=1, replica_groups=mesh['rows'=64,'grp'=4] {'rows','grp'}, dimensions={0} | all-to-all | bytes 262144 | tf_op jit(solution)/shard_map/all_to_all | solution.py:290
  65.9 1.3 %scale.1 = (f32[64,2048]{1,0:T(8,128)}, f32[16,128]{1,0:T(8,128)}, f32[1,1]{1,0:T(1,128)}) custom-call(f32[256,128]{1,0:T(8,128)S(1)} %bitcast.19, f32[16,128]{1,0:T(8,128)S(1)} %get-tuple-element.14.upd_ref, f32[64,2048]{1,0:T(8,128)S(1)} %get-tuple-element.15.held_ref), custom_call_target="tpu_custom_call" | custom-call | tf_op jit(solution)/shard_map/scale/pallas_call | solution.py:270
  (1 shorter events, 0.0 us)
Async XLA Ops:
  0.6 44.4 %copy-start = (bf16[2048,2048]{1,0:T(8,128)(2,1)S(1)}, bf16[2048,2048]{1,0:T(8,128)(2,1)}, u32[]{:S(2)}) copy-start(bf16[2048,2048]{1,0:T(8,128)(2,1)} %vec_ref.1) | copy-start | bytes 25165828
  0.6 44.4 %copy-start.1 = (f32[2048,64]{0,1:T(8,128)S(1)}, f32[2048,64]{0,1:T(8,128)}, u32[]{:S(2)}) copy-start(f32[2048,64]{0,1:T(8,128)} %param.7) | copy-start | bytes 1572868
  0.7 44.4 %copy-start.2 = (f32[2048]{0:T(1024)S(1)}, f32[2048]{0:T(1024)}, u32[]{:S(2)}) copy-start(f32[2048]{0:T(1024)} %param.8) | copy-start | bytes 24580
  26.6 9.6 %collective-permute-start.2 = (f32[32,2176]{1,0:T(8,128)S(1)}, f32[32,2176]{1,0:T(8,128)S(1)}, u32[]{:S(2)}, u32[]{:S(2)}) collective-permute-start(f32[32,2176]{1,0:T(8,128)S(1)} %bitcast.15), channel_id=1, source_target_pairs={{0,3},{1,0},{2,1},{3,2},{4,28},{5,29},{6,30},{7,31},{8,11},{9,8},{... | collective-permute-start | bytes 835592 | tf_op jit(solution)/shard_map/ppermute | solution.py:307
  29.8 7.2 %collective-permute-start.1 = (f32[32,2176]{1,0:T(8,128)S(1)}, f32[32,2176]{1,0:T(8,128)S(1)}, u32[]{:S(2)}, u32[]{:S(2)}) collective-permute-start(f32[32,2176]{1,0:T(8,128)S(1)} %bitcast.16), channel_id=1, source_target_pairs={{0,2},{1,3},{2,0},{3,1},{4,20},{5,21},{6,22},{7,23},{8,10},{9,11},... | collective-permute-start | bytes 835592 | tf_op jit(solution)/shard_map/ppermute | solution.py:307
  29.8 9.9 %collective-permute-start = (f32[32,2176]{1,0:T(8,128)S(1)}, f32[32,2176]{1,0:T(8,128)S(1)}, u32[]{:S(2)}, u32[]{:S(2)}) collective-permute-start(f32[32,2176]{1,0:T(8,128)S(1)} %bitcast.17), channel_id=1, source_target_pairs={{0,1},{1,2},{2,3},{3,0},{4,12},{5,13},{6,14},{7,15},{8,9},{9,10},{... | collective-permute-start | bytes 835592 | tf_op jit(solution)/shard_map/ppermute | solution.py:307
  40.0 5.0 %collective-permute-start.3 = (f32[64,2176]{1,0:T(8,128)S(1)}, f32[64,2176]{1,0:T(8,128)S(1)}, u32[]{:S(2)}, u32[]{:S(2)}) collective-permute-start(f32[64,2176]{1,0:T(8,128)S(1)} %place.1.here_ref), channel_id=1, source_target_pairs={{0,4},{1,5},{2,6},{3,7},{4,0},{5,1},{6,2},{7,3},{8,12},{9,13},{10,... | collective-permute-start | bytes 1671176 | tf_op jit(solution)/shard_map/ppermute | solution.py:310

commit v6 on v5

--- a/solution.py
+++ b/solution.py
@@ -299,7 +299,7 @@
     wide = [at[:, :, 0, x].ravel().tolist() for x in range(shape[3])]
     wide += [at[:, y, 1, :].ravel().tolist() for y in range(shape[1])]
     turns = []
-    for k in range(1, shape[3]):
+    for k in sorted(range(1, shape[3]), key=lambda k: min(k, shape[3] - k)):
         to = np.stack([np.roll(at[:, :, 0], -k, 2), np.roll(at[:, :, 1], -k, 1)], 2)
         turns.append([(int(p), int(q)) for p, q in zip(at.ravel(), to.ravel())])
     mine, plan = pick(pivots[None, :], spb, live, vec, ict, len(wide[0]))

time: 67.3 us -> 66.3 us (0.985)
  waiting for transfers between devices: 10.8 us -> 8.57 us
  blocking collectives: 41.5 us -> 42.3 us
    ppermute x3, waiting for transfers between devices: 9.21 us -> 6.99 us  [on_device(): sheets = [sheet] + [lax.ppermute(sheet, 'd', turn) for turn in turns]]
    all_to_all x2, blocking collectives: 41.5 us -> 42.3 us  [exchange(): lax.all_to_all(blocks, 'd', split_axis=0, concat_axis=0, axis_index_group...]
  transfers between devices with their start and end apart: 4 -> 4, of which waited for: 4 -> 3; matrix products, arithmetic and copies ran while one was open for 0% -> 0% of each run, Pallas kernels for 0% -> 0%
where the time goes in v6:
time: 66.3 us; the launch traced here: 66.2 us
  blocking collectives  42.3 us (64%)
  waiting for transfers between devices  8.57 us (13%)
  starting transfers between devices  7.7 us (12%)
  Pallas kernels  6.88 us (10%)
  between operations  0.69 us (1%)
    all_to_all x2, blocking collectives, exchange(): lax.all_to_all(blocks, 'd', split_axis=0, concat_axis=0, axis_index_group...  42.3 us
    ppermute x3, waiting for transfers between devices, on_device(): sheets = [sheet] + [lax.ppermute(sheet, 'd', turn) for turn in turns]  6.99 us
    ppermute x3, starting transfers between devices, on_device(): sheets = [sheet] + [lax.ppermute(sheet, 'd', turn) for turn in turns]  4.03 us
    ppermute x1, starting transfers between devices, on_device(): other = lax.ppermute(placed, 'd', pairs)  3.67 us
    pallas_call x1, Pallas kernels, step(): pl.pallas_call(step_kernel, out_shape=(pltpu.VMEM((count, rows), F32), pl...  2.87 us
    pallas_call x1, Pallas kernels, pick(): pl.pallas_call(lambda *refs: pick_kernel(count, *refs), out_shape=(jax.Sh...  2.4 us
    ppermute x1, waiting for transfers between devices, on_device(): other = lax.ppermute(placed, 'd', pairs)  1.58 us
  transfers between devices with their start and end apart: 4, of which 3 were waited for; matrix products, arithmetic and copies ran while one was open for 0% of the time, Pallas kernels for 0%

profile of v6, /device:TPU:1, one launch (start us, length us, event | category | flops | bytes accessed | tf_op | source)
XLA Modules:
  0.0 66.2 jit_solution(13701000613673616097)
XLA Ops:
  0.6 0.0 copy-start
  0.6 0.0 copy-start.1
  0.7 0.0 copy-start.2
  0.7 2.4 %pick.1 = (f32[32,1,2176]{2,1,0:T(1,128)S(1)}, s32[34]{0:T(128)S(4)}) custom-call(s32[1,64]{1,0:T(1,128)} %bitcast.22, s32[16]{0:T(128)} %refs_1_.1, s32[16]{0:T(128)} %refs_2_.1, bf16[2048,2048]{1,0:T(8,128)(2,1)} %vec_ref.1, f32[64,2048]{1,0:T(8,128)} %bitcast.13), custom_call_target="tpu_custom_call" | custom-call | tf_op jit(solution)/shard_map/pick/pallas_call | solution.py:100
  3.1 23.5 %all_to_all.16 = f32[32,1,2176]{2,1,0:T(1,128)S(1)} all-to-all(f32[32,1,2176]{2,1,0:T(1,128)S(1)} %get-tuple-element.11), channel_id=1, replica_groups={{0,8,16,24,32,40,48,56,64,72,80,88,96,104,112,120,128,136,144,152,160,1..., dimensions={0} | all-to-all | bytes 557056 | tf_op jit(solution)/shard_map/all_to_all | solution.py:290
  26.6 2.6 %collective-permute-start.2 = (f32[32,2176]{1,0:T(8,128)S(1)}, f32[32,2176]{1,0:T(8,128)S(1)}, u32[]{:S(2)}, u32[]{:S(2)}) collective-permute-start(f32[32,2176]{1,0:T(8,128)S(1)} %bitcast.15), channel_id=1, source_target_pairs={{0,2},{1,3},{2,0},{3,1},{4,20},{5,21},{6,22},{7,23},{8,10},{9,11},... | collective-permute-start | bytes 835592 | tf_op jit(solution)/shard_map/ppermute | solution.py:307
  29.2 0.8 %collective-permute-start.1 = (f32[32,2176]{1,0:T(8,128)S(1)}, f32[32,2176]{1,0:T(8,128)S(1)}, u32[]{:S(2)}, u32[]{:S(2)}) collective-permute-start(f32[32,2176]{1,0:T(8,128)S(1)} %bitcast.16), channel_id=1, source_target_pairs={{0,3},{1,0},{2,1},{3,2},{4,28},{5,29},{6,30},{7,31},{8,11},{9,8},{... | collective-permute-start | bytes 835592 | tf_op jit(solution)/shard_map/ppermute | solution.py:307
  30.0 0.7 %collective-permute-start = (f32[32,2176]{1,0:T(8,128)S(1)}, f32[32,2176]{1,0:T(8,128)S(1)}, u32[]{:S(2)}, u32[]{:S(2)}) collective-permute-start(f32[32,2176]{1,0:T(8,128)S(1)} %bitcast.17), channel_id=1, source_target_pairs={{0,1},{1,2},{2,3},{3,0},{4,12},{5,13},{6,14},{7,15},{8,9},{9,10},{... | collective-permute-start | bytes 835592 | tf_op jit(solution)/shard_map/ppermute | solution.py:307
  30.6 3.0 %collective-permute-done.2.refs_3_ = f32[32,2176]{1,0:T(8,128)S(1)} collective-permute-done((f32[32,2176]{1,0:T(8,128)S(1)}, f32[32,2176]{1,0:T(8,128)S(1)}, u32[]{:S(2)}, u32[]{:S(2)}) %collective-permute-start.2) | collective-permute-done | bytes 278560 | tf_op jit(solution)/shard_map/ppermute | solution.py:307
  33.6 4.0 %collective-permute-done.1.refs_2_ = f32[32,2176]{1,0:T(8,128)S(1)} collective-permute-done((f32[32,2176]{1,0:T(8,128)S(1)}, f32[32,2176]{1,0:T(8,128)S(1)}, u32[]{:S(2)}, u32[]{:S(2)}) %collective-permute-start.1) | collective-permute-done | bytes 278560 | tf_op jit(solution)/shard_map/ppermute | solution.py:307
  37.6 0.0 collective-permute-done.refs_1_
  37.6 0.4 place.1.here_ref
  38.0 3.7 %collective-permute-start.3 = (f32[64,2176]{1,0:T(8,128)S(1)}, f32[64,2176]{1,0:T(8,128)S(1)}, u32[]{:S(2)}, u32[]{:S(2)}) collective-permute-start(f32[64,2176]{1,0:T(8,128)S(1)} %place.1.here_ref), channel_id=1, source_target_pairs={{0,4},{1,5},{2,6},{3,7},{4,0},{5,1},{6,2},{7,3},{8,12},{9,13},{10,... | collective-permute-start | bytes 1671176 | tf_op jit(solution)/shard_map/ppermute | solution.py:310
  41.7 1.6 %collective-permute-done.3.there_ref = f32[64,2176]{1,0:T(8,128)S(1)} collective-permute-done((f32[64,2176]{1,0:T(8,128)S(1)}, f32[64,2176]{1,0:T(8,128)S(1)}, u32[]{:S(2)}, u32[]{:S(2)}) %collective-permute-start.3) | collective-permute-done | bytes 557088 | tf_op jit(solution)/shard_map/ppermute | solution.py:310
  43.2 0.0 copy-done
  43.2 0.0 copy-done.1
  43.2 0.0 copy-done.2
  43.2 2.9 %step.1 = (f32[64,2048]{1,0:T(8,128)S(1)}, f32[16,128]{1,0:T(8,128)S(1)}, f32[256,128]{1,0:T(8,128)S(1)}) custom-call(f32[64,2176]{1,0:T(8,128)S(1)} %place.1.here_ref, f32[64,2176]{1,0:T(8,128)S(1)} %collective-permute-done.3.there_ref, bf16[2048,2048]{1,0:T(8,128)(2,1)S(1)} %copy-done, f32[64,2048]{1,0:T(8,128)S(1)} %bitcast.14, f32[16,128]{1,0:T(8,128)S(1)} %bitcast.21, ...), custom_call_target="tpu_custom_call" | custom-call | tf_op jit(solution)/shard_map/step/pallas_call | solution.py:231
  46.1 18.8 %all_to_all.17 = f32[256,1,128]{2,1,0:T(1,128)S(1)} all-to-all(f32[256,1,128]{2,1,0:T(1,128)S(1)} %bitcast.20), channel_id=1, replica_groups=mesh['rows'=64,'grp'=4] {'rows','grp'}, dimensions={0} | all-to-all | bytes 262144 | tf_op jit(solution)/shard_map/all_to_all | solution.py:290
  64.9 1.3 %scale.1 = (f32[64,2048]{1,0:T(8,128)}, f32[16,128]{1,0:T(8,128)}, f32[1,1]{1,0:T(1,128)}) custom-call(f32[256,128]{1,0:T(8,128)S(1)} %bitcast.19, f32[16,128]{1,0:T(8,128)S(1)} %get-tuple-element.14.upd_ref, f32[64,2048]{1,0:T(8,128)S(1)} %get-tuple-element.15.held_ref), custom_call_target="tpu_custom_call" | custom-call | tf_op jit(solution)/shard_map/scale/pallas_call | solution.py:270
  (1 shorter events, 0.0 us)
Async XLA Ops:
  0.6 42.6 %copy-start = (bf16[2048,2048]{1,0:T(8,128)(2,1)S(1)}, bf16[2048,2048]{1,0:T(8,128)(2,1)}, u32[]{:S(2)}) copy-start(bf16[2048,2048]{1,0:T(8,128)(2,1)} %vec_ref.1) | copy-start | bytes 25165828
  0.6 42.6 %copy-start.1 = (f32[2048,64]{0,1:T(8,128)S(1)}, f32[2048,64]{0,1:T(8,128)}, u32[]{:S(2)}) copy-start(f32[2048,64]{0,1:T(8,128)} %param.7) | copy-start | bytes 1572868
  0.7 42.6 %copy-start.2 = (f32[2048]{0:T(1024)S(1)}, f32[2048]{0:T(1024)}, u32[]{:S(2)}) copy-start(f32[2048]{0:T(1024)} %param.8) | copy-start | bytes 24580
  26.6 7.0 %collective-permute-start.2 = (f32[32,2176]{1,0:T(8,128)S(1)}, f32[32,2176]{1,0:T(8,128)S(1)}, u32[]{:S(2)}, u32[]{:S(2)}) collective-permute-start(f32[32,2176]{1,0:T(8,128)S(1)} %bitcast.15), channel_id=1, source_target_pairs={{0,2},{1,3},{2,0},{3,1},{4,20},{5,21},{6,22},{7,23},{8,10},{9,11},... | collective-permute-start | bytes 835592 | tf_op jit(solution)/shard_map/ppermute | solution.py:307
  29.2 8.5 %collective-permute-start.1 = (f32[32,2176]{1,0:T(8,128)S(1)}, f32[32,2176]{1,0:T(8,128)S(1)}, u32[]{:S(2)}, u32[]{:S(2)}) collective-permute-start(f32[32,2176]{1,0:T(8,128)S(1)} %bitcast.16), channel_id=1, source_target_pairs={{0,3},{1,0},{2,1},{3,2},{4,28},{5,29},{6,30},{7,31},{8,11},{9,8},{... | collective-permute-start | bytes 835592 | tf_op jit(solution)/shard_map/ppermute | solution.py:307
  30.0 7.7 %collective-permute-start = (f32[32,2176]{1,0:T(8,128)S(1)}, f32[32,2176]{1,0:T(8,128)S(1)}, u32[]{:S(2)}, u32[]{:S(2)}) collective-permute-start(f32[32,2176]{1,0:T(8,128)S(1)} %bitcast.17), channel_id=1, source_target_pairs={{0,1},{1,2},{2,3},{3,0},{4,12},{5,13},{6,14},{7,15},{8,9},{9,10},{... | collective-permute-start | bytes 835592 | tf_op jit(solution)/shard_map/ppermute | solution.py:307
  38.0 5.3 %collective-permute-start.3 = (f32[64,2176]{1,0:T(8,128)S(1)}, f32[64,2176]{1,0:T(8,128)S(1)}, u32[]{:S(2)}, u32[]{:S(2)}) collective-permute-start(f32[64,2176]{1,0:T(8,128)S(1)} %place.1.here_ref), channel_id=1, source_target_pairs={{0,4},{1,5},{2,6},{3,7},{4,0},{5,1},{6,2},{7,3},{8,12},{9,13},{10,... | collective-permute-start | bytes 1671176 | tf_op jit(solution)/shard_map/ppermute | solution.py:310
